TPU v7x, 8 devices: a whole 2x2x1 slice. The times are simulated.
8 devices in a mesh: dp: 2 (over z, y), tp: 4 (over x, core).
Axes of the slice: x: 2, y: 2, z: 1, core: 2. Of those that a mesh axis runs over, the one named last changes fastest.
Arguments:
- hidden_in: bfloat16 [2048, 640], P(('dp', 'tp')), parts along dimension 0
- k_cache: bfloat16 [2048, 512, 256], P(('dp', 'tp')), parts along dimension 0
- v_cache: bfloat16 [2048, 512, 256], P(('dp', 'tp')), parts along dimension 0
- cache_len: int32 [2048], P(('dp', 'tp')), parts along dimension 0
- norm_attn: bfloat16 [640], replicated
- norm_mlp: bfloat16 [640], replicated
- w_q: bfloat16 [640, 1024], replicated
- w_k: bfloat16 [640, 256], replicated
- w_v: bfloat16 [640, 256], replicated
- w_o: bfloat16 [1024, 640], replicated
- w_gate: bfloat16 [640, 2048], P(None, 'tp')
- w_up: bfloat16 [640, 2048], P(None, 'tp')
- w_down: bfloat16 [2048, 640], P('tp')
Outputs:
- output 1: bfloat16 [2048, 640], P(('dp', 'tp')), parts along dimension 0
- output 2: bfloat16 [2048, 256], P(('dp', 'tp')), parts along dimension 0
- output 3: bfloat16 [2048, 256], P(('dp', 'tp')), parts along dimension 0
There are 2 independent parts. A program takes and returns all parts, laid end to end along the dimension named above; an argument that names none is the same for every part.
All inputs are finite; a program needn't handle non-finite values.
Results may differ from a plain program's by a relative error of at most 0.00492933.
Values are sent between devices in bfloat16 or wider.
A program may use at most 1 GiB of HBM per device.

v0:
```python
import jax
import jax.numpy as jnp
from jax import lax
from jax.sharding import PartitionSpec as P


def rms_scale(values, gain_vec):
    wide_vals = values.astype(jnp.float32)
    inv_rms = lax.rsqrt(jnp.mean(wide_vals * wide_vals, axis=-1, keepdims=True) + 1e-6)
    return (wide_vals * inv_rms * (1.0 + gain_vec.astype(jnp.float32))).astype(jnp.bfloat16)


def rope_tables(positions, head_dim):
    half_dim = head_dim // 2
    inv_freq = 10000.0 ** (-2.0 * jnp.arange(half_dim, dtype=jnp.float32) / head_dim)
    angles = positions.astype(jnp.float32)[:, None] * inv_freq[None, :]
    return jnp.cos(angles), jnp.sin(angles)


def rotary(values, cos_t, sin_t):
    half_dim = values.shape[-1] // 2
    first_half = values[..., :half_dim]
    second_half = values[..., half_dim:]
    return jnp.concatenate([first_half * cos_t - second_half * sin_t, second_half * cos_t + first_half * sin_t], axis=-1)


def attend(q_rot, k_new, v_new, k_cache, v_cache, cache_len):
    hist_score = jnp.einsum('bhd,btd->bht', q_rot, k_cache, preferred_element_type=jnp.float32)
    new_score = jnp.einsum('bhd,bd->bh', q_rot, k_new, preferred_element_type=jnp.float32)
    valid_mask = lax.broadcasted_iota(jnp.int32, (1, 1, k_cache.shape[1]), 2) < cache_len[:, None, None]
    hist_score = jnp.where(valid_mask, hist_score, -jnp.inf)
    peak_score = jnp.maximum(jnp.max(hist_score, axis=-1), new_score)
    hist_weight = jnp.exp(hist_score - peak_score[..., None])
    new_weight = jnp.exp(new_score - peak_score)
    weight_sum = jnp.sum(hist_weight, axis=-1) + new_weight
    hist_prob = (hist_weight / weight_sum[..., None]).astype(jnp.bfloat16)
    new_prob = (new_weight / weight_sum).astype(jnp.bfloat16)
    attn_out = jnp.einsum('bht,btd->bhd', hist_prob, v_cache, preferred_element_type=jnp.float32)
    attn_out = attn_out + new_prob.astype(jnp.float32)[..., None] * v_new.astype(jnp.float32)[:, None, :]
    return attn_out.astype(jnp.bfloat16)


def attention_block(hidden_in, k_cache, v_cache, cache_len, norm_attn, w_q, w_k, w_v, w_o):
    num_rows = hidden_in.shape[0]
    head_dim = w_k.shape[1]
    num_heads = w_q.shape[1] // head_dim
    normed = rms_scale(hidden_in, norm_attn)
    q_lin = jnp.dot(normed, w_q, preferred_element_type=jnp.float32).reshape(num_rows, num_heads, head_dim)
    k_lin = jnp.dot(normed, w_k, preferred_element_type=jnp.float32)
    v_new = jnp.dot(normed, w_v, preferred_element_type=jnp.float32).astype(jnp.bfloat16)
    cos_t, sin_t = rope_tables(cache_len, head_dim)
    q_rot = (rotary(q_lin, cos_t[:, None, :], sin_t[:, None, :]) * head_dim ** -0.5).astype(jnp.bfloat16)
    k_new = rotary(k_lin, cos_t, sin_t).astype(jnp.bfloat16)
    attn_out = attend(q_rot, k_new, v_new, k_cache, v_cache, cache_len)
    mixed = jnp.dot(attn_out.reshape(num_rows, num_heads * head_dim), w_o, preferred_element_type=jnp.float32)
    return hidden_in.astype(jnp.float32) + mixed, k_new, v_new


def solution(mesh):
    row_spec = P(('dp', 'tp'), None)
    cache_spec = P(('dp', 'tp'), None, None)
    full_vec = P(None)
    full_mat = P(None, None)

    def per_device(hidden_in, k_cache, v_cache, cache_len, norm_attn, norm_mlp, w_q, w_k, w_v, w_o, w_gate, w_up, w_down):
        x_mid, k_new, v_new = attention_block(hidden_in, k_cache, v_cache, cache_len, norm_attn, w_q, w_k, w_v, w_o)
        xn_mid = rms_scale(x_mid, norm_mlp)
        group_rows = lax.all_gather(xn_mid, 'tp', axis=0, tiled=True)
        gate_act = jnp.dot(group_rows, w_gate, preferred_element_type=jnp.float32)
        up_act = jnp.dot(group_rows, w_up, preferred_element_type=jnp.float32)
        hidden_act = (jax.nn.gelu(gate_act, approximate=True) * up_act).astype(jnp.bfloat16)
        part_sum = jnp.dot(hidden_act, w_down, preferred_element_type=jnp.float32)
        down_sum = lax.psum_scatter(part_sum, 'tp', scatter_dimension=0, tiled=True)
        return (x_mid + down_sum).astype(jnp.bfloat16), k_new, v_new

    return jax.shard_map(
        per_device,
        mesh=mesh,
        in_specs=(row_spec, cache_spec, cache_spec, P(('dp', 'tp')), full_vec, full_vec,
                  full_mat, full_mat, full_mat, full_mat, P(None, 'tp'), P(None, 'tp'), P('tp', None)),
        out_specs=(row_spec, row_spec, row_spec),
        check_vma=False,
    )
```

profile of v0, /device:TPU:0, one launch (start us, length us, event | category | flops | bytes accessed | tf_op | source)
XLA Modules:
  0.0 142.6 jit_solution(5666307576309402144)
XLA Ops:
  7.3 0.8 convert_element_type.50
  8.1 0.8 iota_compare_fusion
  8.9 1.1 fusion.21
  10.0 0.7 convert_add_fusion.1
  10.7 0.7 convert_add_fusion
  11.4 1.5 %fusion.33 = f32[256,256]{0,1:T(8,128)S(1)} fusion(bf16[640,256]{1,0:T(8,128)(2,1)} %param.20, bf16[256,640]{1,0:T(8,128)(2,1)} %param.13, f32[640]{0:T(1024)S(1)} %convert_add_fusion.1, f32[256]{0:T(256)S(1)} %add_rsqrt_fusion.1), kind=kOutput, calls=%fused_computation.60 | convolution fusion | flops 84541440 | bytes 921088 | tf_op jit(solution)/shard_map/dot_general | solution.py:49
  12.9 0.6 subtract_convert_fusion
  13.4 0.8 copy.17
  14.2 0.7 copy.16
  14.9 0.7 pad_maximum_fusion
  15.6 0.9 copy.19
  16.5 1.1 fusion.37
  17.5 0.6 fusion.35
  18.2 0.5 reshape.105
  18.7 1.3 multiply_subtract_fusion
  20.0 0.3 fusion.12
  20.3 0.4 fusion.38
  20.7 25.6 %select_reduce_fusion = (f32[256,4]{1,0:T(8,128)S(1)}, f32[256,4,512]{2,1,0:T(4,128)S(1)}) fusion(pred[256,512]{1,0:T(8,128)(4,1)S(1)} %iota_compare_fusion, bf16[256,4,256]{2,1,0:T(4,128)(2,1)S(1)} %fusion.12, bf16[256,512,256]{2,1,0:T(8,128)(2,1)} %param.14), kind=kOutput, calls=%fused_computation.12 | convolution fusion | flops 269483008 | bytes 69865472 | tf_op jit(solution)/shard_map/bhd,btd->bht/dot_general | solution.py:28
  46.3 1.6 %fusion.9 = f32[256,4]{1,0:T(8,128)S(1)} fusion(f32[256,4,512]{2,1,0:T(4,128)S(1)} %get-tuple-element.17, f32[256,4]{1,0:T(8,128)S(1)} %max.3, pred[256,512]{1,0:T(8,128)(4,1)S(1)} %iota_compare_fusion), kind=kLoop, calls=%fused_computation.14 | loop fusion | flops 1571840 | bytes 2236416 | tf_op jit(solution)/shard_map/reduce_sum | solution.py:35
  48.0 0.7 fusion.24
  48.7 24.8 %fusion.10 = bf16[256,4,256]{2,1,0:T(4,128)(2,1)} fusion(bf16[256,512,256]{2,1,0:T(8,128)(2,1)} %param.15, f32[256,4,512]{2,1,0:T(4,128)S(1)} %get-tuple-element.17, f32[256,4]{1,0:T(8,128)} %get-tuple-element.9, f32[256,4]{1,0:T(8,128)} %copy-done.2, pred[256,512]{1,0:T(8,128)(4,1)S(1)} %iota_compare_fusion, f32[256,256]{1,0:T(8,128)} %get-tuple-element.18, ...), kind=kOutput, calls=%fused_computation.15 | convolution fusion | flops 271319040 | bytes 70135808 | tf_op jit(solution)/shard_map/bht,btd->bhd/dot_general | solution.py:38
  73.5 1.1 copy.21
  74.6 2.0 %multiply_reduce_fusion = (f32[256]{0:T(256)S(1)}, f32[256,640]{1,0:T(8,128)S(1)}) fusion(bf16[256,1024]{1,0:T(8,128)(2,1)S(1)} %bitcast.22, bf16[1024,640]{1,0:T(8,128)(2,1)} %param.22, bf16[256,640]{1,0:T(8,128)(2,1)} %param.13), kind=kOutput, calls=%fused_computation.36 | convolution fusion | flops 336199424 | bytes 2819072 | tf_op jit(solution)/shard_map/dot_general | solution.py:55
  76.7 0.9 multiply_convert_fusion
  77.6 0.2 reduce-scatter.2.cloned.1.call-start
  77.8 17.9 %all-gather.2.cloned.1.call-done = bf16[1024,640]{1,0:T(8,128)(2,1)} async-done(((bf16[256,640]{1,0:T(8,128)(2,1)}), bf16[1024,640]{1,0:T(8,128)(2,1)}) %all-gather.2.cloned.1.call-update) | async-done | bytes 1310736 | tf_op jit(solution)/shard_map/all_gather | solution.py:68
  95.7 3.9 %fusion.39 = f32[1024,512]{1,0:T(8,128)} fusion(bf16[1024,640]{1,0:T(8,128)(2,1)} %all-gather.2.cloned.1.call-done, bf16[640,512]{1,0:T(8,128)(2,1)} %param.23), kind=kOutput, calls=%fused_computation.64 | convolution fusion | flops 671088640 | bytes 4063232 | tf_op jit(solution)/shard_map/dot_general | solution.py:69
  99.6 5.4 %fusion.11 = f32[1024,640]{1,0:T(8,128)} fusion(bf16[512,640]{1,0:T(8,128)(2,1)} %param.25, f32[1024,512]{1,0:T(8,128)} %fusion.39, bf16[1024,640]{1,0:T(8,128)(2,1)S(1)} %copy-done.6, bf16[640,512]{1,0:T(8,128)(2,1)} %param.24), kind=kOutput, calls=%fused_computation.17 | convolution fusion | flops 1347420160 | bytes 7340032 | tf_op jit(solution)/shard_map/dot_general | solution.py:72
  105.0 0.9 copy-done.3
  105.9 0.8 copy.18
  106.7 27.2 %reduce-scatter.2.cloned.1.call-done = f32[256,640]{1,0:T(8,128)} async-done(((f32[1024,640]{1,0:T(8,128)}), f32[256,640]{1,0:T(8,128)}) %reduce-scatter.2.cloned.1.call-update) | async-done | bytes 655376 | tf_op jit(solution)/shard_map/reduce_scatter | solution.py:73
  133.9 1.9 %add_convert_fusion = bf16[256,640]{1,0:T(8,128)(2,1)} fusion(f32[256,640]{1,0:T(8,128)S(1)} %get-tuple-element.21, f32[256,640]{1,0:T(8,128)} %reduce-scatter.2.cloned.1.call-done), kind=kLoop, calls=%fused_computation.34 | loop fusion | flops 327680 | bytes 1638400 | tf_op jit(solution)/shard_map/convert_element_type | solution.py:74
  (20 shorter events, 0.2 us)
Async XLA Ops:
  7.2 10.4 %copy-start = (bf16[640,1024]{1,0:T(8,128)(2,1)S(1)}, bf16[640,1024]{1,0:T(8,128)(2,1)}, u32[]{:S(2)}) copy-start(bf16[640,1024]{1,0:T(8,128)(2,1)} %param.19) | copy-start | bytes 3932164
  7.2 9.3 %copy-start.1 = (bf16[256,640]{1,0:T(8,128)(2,1)S(1)}, bf16[256,640]{1,0:T(8,128)(2,1)}, u32[]{:S(2)}) copy-start(bf16[256,640]{1,0:T(8,128)(2,1)} %param.13) | copy-start | bytes 983044
  7.2 9.3 %copy-start.4 = (bf16[640,256]{1,0:T(8,128)(2,1)S(1)}, bf16[640,256]{1,0:T(8,128)(2,1)}, u32[]{:S(2)}) copy-start(bf16[640,256]{1,0:T(8,128)(2,1)} %param.21) | copy-start | bytes 983044
  7.2 88.5 %all-gather.2.cloned.1.call-start = ((), (), s32[]{:S(2)}) async-start(), calls=%async_computation.1 | async-start | bytes 1638400 | tf_op jit(solution)/shard_map/all_gather | solution.py:68
  18.7 1.6 %copy-start.5 = (bf16[256,256,1]{1,2,0:T(2,128)(2,1)S(1)}, bf16[256,256,1]{1,2,0:T(2,128)(2,1)}, u32[]{:S(2)}) copy-start(bf16[256,256,1]{1,2,0:T(2,128)(2,1)} %copy.19) | copy-start | bytes 393220
  46.3 1.6 %copy-start.2 = (f32[256,4]{1,0:T(8,128)}, f32[256,4]{1,0:T(8,128)S(1)}, u32[]{:S(2)}) copy-start(f32[256,4]{1,0:T(8,128)S(1)} %max.3) | copy-start | bytes 12292
  77.6 56.3 %reduce-scatter.2.cloned.1.call-start = ((), (), s32[]{:S(2)}) async-start(), calls=%async_computation.2 | async-start | bytes 3276800 | tf_op jit(solution)/shard_map/reduce_scatter | solution.py:73
  95.7 3.9 %copy-start.6 = (bf16[1024,640]{1,0:T(8,128)(2,1)S(1)}, bf16[1024,640]{1,0:T(8,128)(2,1)}, u32[]{:S(2)}) copy-start(bf16[1024,640]{1,0:T(8,128)(2,1)} %all-gather.2.cloned.1.call-done) | copy-start | bytes 3932164
  105.0 0.9 copy-start.3
Sparse Core Ops, SparseCore 0:
  77.7 17.9 all-gather.1
  105.2 28.6 reduce-scatter.1
where the time goes:
time: 143 us
  matrix products  65.3 us (46%)
  waiting for transfers between devices  45.2 us (32%)
  between operations  14.2 us (10%)
  other arithmetic  12 us (8%)
  local copies, waits for them, and re-layouts  5.66 us (4%)
    reduce_scatter x1, waiting for transfers between devices, per_device(): down_sum = lax.psum_scatter(part_sum, 'tp', scatter_dimension=0, tiled=True)  27.2 us
    dot_general x1, matrix products, attend(): jnp.einsum('bhd,btd->bht', q_rot, k_cache, preferred_element_type=jnp.flo...  25.6 us
    dot_general x1, matrix products, attend(): jnp.einsum('bht,btd->bhd', hist_prob, v_cache, preferred_element_type=jnp...  24.8 us
    all_gather x1, waiting for transfers between devices, per_device(): group_rows = lax.all_gather(xn_mid, 'tp', axis=0, tiled=True)  17.9 us
    dot_general x1, matrix products, per_device(): part_sum = jnp.dot(hidden_act, w_down, preferred_element_type=jnp.float32)  5.38 us
    dot_general x1, matrix products, per_device(): gate_act = jnp.dot(group_rows, w_gate, preferred_element_type=jnp.float32)  3.89 us
  transfers between devices with their start and end apart: 2, of which 2 were waited for; matrix products, arithmetic and copies ran while one was open for 1% of the time, Pallas kernels for 0%

commit v1 on v0

v1 whole, which is shorter than its diff:
```python
import functools

import jax
import jax.numpy as jnp
from jax import lax
from jax.experimental import pallas as pl
from jax.experimental.pallas import tpu as pltpu
from jax.sharding import PartitionSpec as P

HEADS = 4
HEAD_DIM = 256
HALF = HEAD_DIM // 2
GROUP = 8
RING = 8
BLOCK = 128
F32 = jnp.float32
BF16 = jnp.bfloat16


def rms_scale(values, gain_vec):
    wide_vals = values.astype(F32)
    inv_rms = lax.rsqrt(jnp.mean(wide_vals * wide_vals, axis=-1, keepdims=True) + 1e-6)
    return (wide_vals * inv_rms * (1.0 + gain_vec.astype(F32))).astype(BF16)


def dot(a, b):
    return jnp.dot(a, b, preferred_element_type=F32)


def dot_t(a, b):
    return lax.dot_general(a, b, (((1,), (1,)), ((), ())), preferred_element_type=F32)


def attn_kernel(rows, cache_size, x_ref, len_ref, na_ref, nm_ref, wq_ref, wk_ref, wv_ref, wo_ref, freq_ref, k_hbm, v_hbm,
                x1_ref, xn2_ref, knew_ref, vnew_ref,
                kbuf, vbuf, qg, ks, vs, lensb, s_buf, o_s, table, table_s, ksem, vsem, tsem):
    groups = rows // GROUP
    max_nb = cache_size // BLOCK

    len_row = len_ref[...].astype(F32)
    lane_id = lax.broadcasted_iota(jnp.int32, (1, rows), 1).astype(F32)
    key_row = len_row * rows + (rows - 1 - lane_id)
    key_col = jnp.broadcast_to(key_row, (128, rows)).T[:, :1]
    len_col = jnp.broadcast_to(len_row, (128, rows)).T[:, :1]
    sub_id = lax.broadcasted_iota(jnp.int32, (rows, rows), 0).astype(F32)
    lane_sq = lax.broadcasted_iota(jnp.int32, (rows, rows), 1).astype(F32)
    rank_row = jnp.sum((key_col > key_row).astype(F32), axis=0, keepdims=True)
    rank_col = jnp.sum((key_row > key_col).astype(F32), axis=1, keepdims=True)
    to_sorted = rank_row == sub_id
    to_natural = rank_col == lane_sq
    perm_row = jnp.sum(jnp.where(to_natural, sub_id, 0.0), axis=0, keepdims=True)
    slen_row = jnp.sum(jnp.where(to_natural, len_col, 0.0), axis=0, keepdims=True)
    slen_col = jnp.sum(jnp.where(to_sorted, len_row, 0.0), axis=1, keepdims=True)
    table[0:1, :] = (perm_row + rows * slen_row).astype(jnp.int32)
    table_copy = pltpu.make_async_copy(table.at[0:1], table_s, tsem)
    table_copy.start()
    lensb[...] = jnp.broadcast_to(slen_col, (rows, 128))

    zero = jnp.zeros((cache_size, HEAD_DIM), BF16)

    def clear(i, c):
        kbuf[i] = zero
        vbuf[i] = zero
        return c
    lax.fori_loop(0, RING * GROUP, clear, 0)
    table_copy.wait()

    def entry(pos):
        packed = table_s[0, pos]
        row = lax.rem(packed, rows)
        length = lax.div(packed, rows)
        size = jnp.maximum(lax.div(length + 15, 16) * 16, 16)
        return row, length, pl.multiple_of(size, 16)

    def k_copy(pos):
        row, _, size = entry(pos)
        slot = lax.rem(pos, RING * GROUP)
        return pltpu.make_async_copy(k_hbm.at[row, pl.ds(0, size)], kbuf.at[slot, pl.ds(0, size)], ksem.at[slot])

    def v_copy(pos):
        row, _, size = entry(pos)
        slot = lax.rem(pos, RING * GROUP)
        return pltpu.make_async_copy(v_hbm.at[row, pl.ds(0, size)], vbuf.at[slot, pl.ds(0, size)], vsem.at[slot])

    def issue(g):
        for b in range(GROUP):
            k_copy(g * GROUP + b).start()
            v_copy(g * GROUP + b).start()

    def wait_k(g):
        for b in range(GROUP):
            k_copy(g * GROUP + b).wait()

    def wait_v(g):
        for b in range(GROUP):
            v_copy(g * GROUP + b).wait()

    def prologue(g, c):
        issue(g)
        return c
    lax.fori_loop(0, RING, prologue, 0)

    xn = rms_scale(x_ref[...], na_ref[...])
    angles = len_col * freq_ref[...]
    cos_t, sin_t = jnp.cos(angles), jnp.sin(angles)

    def rotary(val):
        first, second = val[:, :HALF], val[:, HALF:]
        return jnp.concatenate([first * cos_t - second * sin_t, second * cos_t + first * sin_t], axis=-1)

    pick = to_sorted.astype(BF16)
    k_bf = rotary(dot(xn, wk_ref[...])).astype(BF16)
    v_bf = dot(xn, wv_ref[...]).astype(BF16)
    knew_ref[...] = k_bf
    vnew_ref[...] = v_bf
    ks[...] = dot(pick, k_bf)
    vs[...] = dot(pick, v_bf)
    for h in range(HEADS):
        q_h = (rotary(dot(xn, wq_ref[:, h * HEAD_DIM:(h + 1) * HEAD_DIM])) * HEAD_DIM ** -0.5).astype(BF16)
        q_s = dot(pick, q_h)
        qg[0:groups, h * GROUP:(h + 1) * GROUP, :] = q_s.reshape(groups, GROUP, HEAD_DIM)
    qg[groups] = jnp.zeros((HEADS * GROUP, HEAD_DIM), F32)

    def scores(g, nb):
        base = lax.rem(g, RING) * GROUP
        q = qg[g].astype(BF16)
        member = lax.broadcasted_iota(jnp.int32, (HEADS * GROUP, HEAD_DIM), 0) % GROUP
        out = None
        for b in range(GROUP):
            part = dot_t(jnp.where(member == b, q, jnp.zeros_like(q)), kbuf[base + b, :nb * BLOCK, :])
            out = part if out is None else out + part
        return out

    def finish(g, nb):
        width = nb * BLOCK
        base = lax.rem(g, RING) * GROUP
        start = pl.multiple_of(g * GROUP, GROUP)
        tile4 = lambda t: jnp.concatenate([t] * HEADS, axis=0)
        s = s_buf[:, :width]
        lens = tile4(lensb[pl.ds(start, GROUP), :])[:, :1]
        valid = lax.broadcasted_iota(jnp.int32, (HEADS * GROUP, width), 1).astype(F32) < lens
        q = qg[g]
        s_new = jnp.sum(q * tile4(ks[pl.ds(start, GROUP), :]), axis=-1, keepdims=True)
        s = jnp.where(valid, s, -jnp.inf)
        peak = jnp.maximum(jnp.max(s, axis=-1, keepdims=True), s_new)
        w = jnp.exp(s - peak)
        w_new = jnp.exp(s_new - peak)
        inv = 1.0 / (jnp.sum(w, axis=-1, keepdims=True) + w_new)
        prob = (w * inv).astype(BF16)
        prob_new = (w_new * inv).astype(BF16).astype(F32)
        member = lax.broadcasted_iota(jnp.int32, (HEADS * GROUP, width), 0) % GROUP
        out = None
        for b in range(GROUP):
            part = dot(jnp.where(member == b, prob, jnp.zeros_like(prob)), vbuf[base + b, :width, :])
            out = part if out is None else out + part
        out = out + prob_new * tile4(vs[pl.ds(start, GROUP), :])
        for h in range(HEADS):
            o_s[pl.ds(start, GROUP), h * HEAD_DIM:(h + 1) * HEAD_DIM] = out[h * GROUP:(h + 1) * GROUP]

    def blocks(g):
        length = lax.div(table_s[0, g * GROUP], rows)
        return jnp.maximum(lax.div(length + BLOCK - 1, BLOCK), 1)

    wait_k(0)
    s_buf[...] = scores(0, max_nb)

    def step(g, c):
        @pl.when(jnp.logical_and(g >= 1, g + RING - 1 < groups))
        def _():
            issue(g + RING - 1)
        wait_v(g)

        @pl.when(g + 1 < groups)
        def _():
            wait_k(g + 1)
        nb_g = blocks(g)
        for nb in range(1, max_nb + 1):
            @pl.when(nb_g == nb)
            def _():
                nxt = scores(g + 1, nb)
                finish(g, nb)
                s_buf[:, :nb * BLOCK] = nxt
        return c
    lax.fori_loop(0, groups, step, 0)

    back = to_natural.astype(BF16)
    mixed = None
    for h in range(HEADS):
        o_h = dot(back, o_s[:, h * HEAD_DIM:(h + 1) * HEAD_DIM].astype(BF16)).astype(BF16)
        part = dot(o_h, wo_ref[h * HEAD_DIM:(h + 1) * HEAD_DIM, :])
        mixed = part if mixed is None else mixed + part
    x1 = x_ref[...].astype(F32) + mixed
    x1_ref[...] = x1
    xn2_ref[...] = rms_scale(x1, nm_ref[...])


def attention(hidden_in, k_cache, v_cache, cache_len, norm_attn, norm_mlp, w_q, w_k, w_v, w_o):
    rows, d_model = hidden_in.shape
    cache_size = k_cache.shape[1]
    groups = rows // GROUP
    freq = 10000.0 ** (-2.0 * jnp.arange(HALF, dtype=F32) / HEAD_DIM)
    vmem = pl.BlockSpec(memory_space=pltpu.VMEM)
    hbm = pl.BlockSpec(memory_space=pl.ANY)
    return pl.pallas_call(
        functools.partial(attn_kernel, rows, cache_size),
        out_shape=(jax.ShapeDtypeStruct((rows, d_model), F32), jax.ShapeDtypeStruct((rows, d_model), BF16),
                   jax.ShapeDtypeStruct((rows, HEAD_DIM), BF16), jax.ShapeDtypeStruct((rows, HEAD_DIM), BF16)),
        in_specs=[vmem] * 9 + [hbm] * 2,
        out_specs=(vmem,) * 4,
        scratch_shapes=[
            pltpu.VMEM((RING * GROUP, cache_size, HEAD_DIM), BF16),
            pltpu.VMEM((RING * GROUP, cache_size, HEAD_DIM), BF16),
            pltpu.VMEM((groups + 1, HEADS * GROUP, HEAD_DIM), F32),
            pltpu.VMEM((rows, HEAD_DIM), F32),
            pltpu.VMEM((rows, HEAD_DIM), F32),
            pltpu.VMEM((rows, 128), F32),
            pltpu.VMEM((HEADS * GROUP, cache_size), F32),
            pltpu.VMEM((rows, HEADS * HEAD_DIM), F32),
            pltpu.VMEM((8, rows), jnp.int32),
            pltpu.SMEM((1, rows), jnp.int32),
            pltpu.SemaphoreType.DMA((RING * GROUP,)),
            pltpu.SemaphoreType.DMA((RING * GROUP,)),
            pltpu.SemaphoreType.DMA,
        ],
        compiler_params=pltpu.CompilerParams(vmem_limit_bytes=52 * 1024 * 1024),
        cost_estimate=pl.CostEstimate(flops=10 ** 10, bytes_accessed=7 * 10 ** 7, transcendentals=10 ** 6),
        name='attention',
    )(hidden_in, cache_len.reshape(1, rows), norm_attn.reshape(1, d_model), norm_mlp.reshape(1, d_model),
      w_q, w_k, w_v, w_o, freq.reshape(1, HALF), k_cache, v_cache)


CORE = [(0, 1), (1, 0), (2, 3), (3, 2)]
ACROSS = [(0, 2), (1, 3), (2, 0), (3, 1)]


def solution(mesh):
    row_spec = P(('dp', 'tp'), None)
    cache_spec = P(('dp', 'tp'), None, None)
    full_vec = P(None)
    full_mat = P(None, None)

    def per_device(hidden_in, k_cache, v_cache, cache_len, norm_attn, norm_mlp, w_q, w_k, w_v, w_o, w_gate, w_up, w_down):
        own = (w_gate, w_up, w_down)
        far = tuple(lax.ppermute(w, 'tp', ACROSS) for w in own)
        near = tuple(lax.ppermute(w, 'tp', CORE) for w in own)
        x_mid, xn_mid, k_new, v_new = attention(hidden_in, k_cache, v_cache, cache_len, norm_attn, norm_mlp, w_q, w_k, w_v, w_o)
        diag = tuple(lax.ppermute(w, 'tp', CORE) for w in far)
        total = x_mid
        for gate, up, down in (own, near, far, diag):
            gate_act = dot(xn_mid, gate)
            up_act = dot(xn_mid, up)
            hidden_act = (jax.nn.gelu(gate_act, approximate=True) * up_act).astype(BF16)
            total = total + dot(hidden_act, down)
        return total.astype(BF16), k_new, v_new

    return jax.shard_map(
        per_device,
        mesh=mesh,
        in_specs=(row_spec, cache_spec, cache_spec, P(('dp', 'tp')), full_vec, full_vec,
                  full_mat, full_mat, full_mat, full_mat, P(None, 'tp'), P(None, 'tp'), P('tp', None)),
        out_specs=(row_spec, row_spec, row_spec),
        check_vma=False,
    )
```

time: 143 us -> 72.1 us (0.50)
  matrix products: 65.3 us -> 13.8 us
  Pallas kernels: 0 us -> 45.6 us
  waiting for transfers between devices: 45.2 us -> 0.02 us
  between operations: 14.2 us -> 0.77 us
  other arithmetic: 12 us -> 0.01 us
  starting transfers between devices: 0.26 us -> 6.67 us
    dot_general x9 -> x8, matrix products: 65.3 us -> 13.8 us  [dot(): return jnp.dot(a, b, preferred_element_type=F32)]
    pallas_call x0 -> x1, Pallas kernels: none -> 45.6 us  [attention(): pl.pallas_call(functools.partial(attn_kernel, rows, cache_size), out_shap...]
    reduce_scatter x1 -> x0, waiting for transfers between devices: 27.2 us -> none  [per_device(): down_sum = lax.psum_scatter(part_sum, 'tp', scatter_dimension=0, tiled=True)]
    all_gather x1 -> x0, waiting for transfers between devices: 17.9 us -> none  [per_device(): group_rows = lax.all_gather(xn_mid, 'tp', axis=0, tiled=True)]
    ppermute x0 -> x9, starting transfers between devices: none -> 6.67 us  [the longest x3 5.18 us: per_device(): far = tuple((lax.ppermute(w, 'tp', ACROSS) for w in own))]
    convert_element_type x5 -> x0, other arithmetic: 4.57 us -> none  [the longest x1 1.87 us: per_device(): return ((x_mid + down_sum).astype(jnp.bfloat16), k_new, v_new)]
    reduce_sum x2 -> x0, other arithmetic: 2.72 us -> none  [the longest x1 1.61 us: attend(): weight_sum = jnp.sum(hist_weight, axis=-1) + new_weight]
    unnamed x16 -> x12, local copies, waits for them, and re-layouts: 2.8 us -> 3.6 us
  transfers between devices with their start and end apart: 2 -> 9, of which waited for: 2 -> 0; matrix products, arithmetic and copies ran while one was open for 1% -> 17% of each run, Pallas kernels for 0% -> 63%
where the time goes in v1:
time: 72.1 us; the launch traced here: 71.8 us
  Pallas kernels  45.6 us (63%)
  matrix products  13.8 us (19%)
  starting transfers between devices  6.67 us (9%)
  local copies, waits for them, and re-layouts  4.98 us (7%)
  between operations  0.77 us (1%)
    pallas_call x1, Pallas kernels, attention(): pl.pallas_call(functools.partial(attn_kernel, rows, cache_size), out_shap...  45.6 us
    dot_general x8, matrix products, dot(): return jnp.dot(a, b, preferred_element_type=F32)  13.8 us
    ppermute x3, starting transfers between devices, per_device(): far = tuple((lax.ppermute(w, 'tp', ACROSS) for w in own))  5.18 us
    unnamed x12, local copies, waits for them, and re-layouts  3.6 us
  transfers between devices with their start and end apart: 9, of which 0 were waited for; matrix products, arithmetic and copies ran while one was open for 17% of the time, Pallas kernels for 63%

profile of v1, /device:TPU:0, one launch (start us, length us, event | category | flops | bytes accessed | tf_op | source)
XLA Modules:
  0.0 71.8 jit_solution(7736870618834471321)
XLA Ops:
  0.6 3.4 %collective-permute-start.3 = (bf16[640,512]{1,0:T(8,128)(2,1)}, bf16[640,512]{1,0:T(8,128)(2,1)}, u32[]{:S(2)}, u32[]{:S(2)}) collective-permute-start(bf16[640,512]{1,0:T(8,128)(2,1)} %param.23), channel_id=1, source_target_pairs={{0,2},{1,3},{2,0},{3,1},{4,6},{5,7},{6,4},{7,5}} | collective-permute-start | bytes 1966088 | tf_op jit(solution)/shard_map/ppermute | solution.py:244
  4.0 0.0 collective-permute-start
  4.0 0.1 collective-permute-start.4
  4.1 0.4 collective-permute-start.1
  4.5 1.7 %collective-permute-start.5 = (bf16[512,640]{1,0:T(8,128)(2,1)}, bf16[512,640]{1,0:T(8,128)(2,1)}, u32[]{:S(2)}, u32[]{:S(2)}) collective-permute-start(bf16[512,640]{1,0:T(8,128)(2,1)} %param.25), channel_id=1, source_target_pairs={{0,2},{1,3},{2,0},{3,1},{4,6},{5,7},{6,4},{7,5}} | collective-permute-start | bytes 1966088 | tf_op jit(solution)/shard_map/ppermute | solution.py:244
  6.3 0.7 reshape.27.na_ref
  7.0 0.7 reshape.28.nm_ref
  7.6 1.0 %copy-done = bf16[256,640]{1,0:T(8,128)(2,1)S(1)} copy-done((bf16[256,640]{1,0:T(8,128)(2,1)S(1)}, bf16[256,640]{1,0:T(8,128)(2,1)}, u32[]{:S(2)}) %copy-start) | copy-done | bytes 327704
  8.6 1.0 %copy-done.1 = bf16[640,256]{1,0:T(8,128)(2,1)S(1)} copy-done((bf16[640,256]{1,0:T(8,128)(2,1)S(1)}, bf16[640,256]{1,0:T(8,128)(2,1)}, u32[]{:S(2)}) %copy-start.1) | copy-done | bytes 327704
  9.6 1.0 %copy-done.2 = bf16[640,256]{1,0:T(8,128)(2,1)S(1)} copy-done((bf16[640,256]{1,0:T(8,128)(2,1)S(1)}, bf16[640,256]{1,0:T(8,128)(2,1)}, u32[]{:S(2)}) %copy-start.2) | copy-done | bytes 327704
  10.6 0.7 copy-done.3
  11.2 45.6 %attention.1 = (f32[256,640]{1,0:T(8,128)S(1)}, bf16[256,640]{1,0:T(8,128)(2,1)S(1)}, bf16[256,256]{1,0:T(8,128)(2,1)}, bf16[256,256]{1,0:T(8,128)(2,1)}) custom-call(bf16[256,640]{1,0:T(8,128)(2,1)S(1)} %copy-done, s32[1,256]{1,0:T(1,128)S(1)} %bitcast.21, bf16[1,640]{1,0:T(2,128)(2,1)S(1)} %reshape.27.na_ref, bf16[1,640]{1,0:T(2,128)(2,1)S(1)} %reshape.28.nm_ref, ...), custom_call_target="tpu_custom_call" | custom-call | flops 10000000000 | bytes 70000000 | tf_op jit(solution)/shard_map/attention/pallas_call | solution.py:204
  56.8 0.4 fusion.80
  57.2 1.8 %convolution_add_fusion.2 = f32[256,640]{1,0:T(8,128)S(1)} fusion(f32[256,640]{1,0:T(8,128)S(1)} %get-tuple-element.7, bf16[512,640]{1,0:T(8,128)(2,1)} %param.25, bf16[256,640]{1,0:T(8,128)(2,1)S(1)} %get-tuple-element.8, bf16[640,512]{1,0:T(8,128)(2,1)S(1)} %copy-done.5, f32[256,512]{1,0:T(8,128)S(1)} %fusion.80), kind=kOutput, calls=%fused_computation.2 | convolution fusion | flops 337018880 | bytes 3473408 | tf_op jit(solution)/shard_map/dot_general | solution.py:27
  59.0 0.0 collective-permute-done.3
  59.0 0.0 collective-permute-start.2
  59.0 1.4 %fusion.82 = f32[256,512]{1,0:T(8,128)S(1)} fusion(bf16[256,640]{1,0:T(8,128)(2,1)S(1)} %get-tuple-element.8, bf16[640,512]{1,0:T(8,128)(2,1)} %collective-permute-done.3), kind=kOutput, calls=%fused_computation.84 | convolution fusion | flops 167772160 | bytes 1507328 | tf_op jit(solution)/shard_map/dot_general | solution.py:27
  60.5 0.0 collective-permute-done.4
  60.5 0.5 collective-permute-start.6
  61.0 0.0 collective-permute-done.5
  61.0 0.0 collective-permute-start.7
  61.1 2.8 %fusion.39 = f32[256,640]{1,0:T(8,128)} fusion(bf16[512,640]{1,0:T(8,128)(2,1)} %collective-permute-done.5, f32[256,512]{1,0:T(8,128)S(1)} %fusion.82, bf16[256,640]{1,0:T(8,128)(2,1)S(1)} %get-tuple-element.8, bf16[640,512]{1,0:T(8,128)(2,1)} %collective-permute-done.4), kind=kOutput, calls=%fused_computation.45 | convolution fusion | flops 336855040 | bytes 2818048 | tf_op jit(solution)/shard_map/dot_general | solution.py:27
  63.9 0.0 collective-permute-done
  63.9 0.5 collective-permute-start.8
  64.4 1.4 %fusion.81 = f32[256,512]{1,0:T(8,128)S(1)} fusion(bf16[256,640]{1,0:T(8,128)(2,1)S(1)} %get-tuple-element.8, bf16[640,512]{1,0:T(8,128)(2,1)} %collective-permute-done), kind=kOutput, calls=%fused_computation.83 | convolution fusion | flops 167772160 | bytes 1507328 | tf_op jit(solution)/shard_map/dot_general | solution.py:27
  65.8 0.0 collective-permute-done.1
  65.8 0.0 collective-permute-done.2
  65.8 1.8 %fusion = f32[256,640]{1,0:T(8,128)S(1)} fusion(f32[256,640]{1,0:T(8,128)} %fusion.39, f32[256,640]{1,0:T(8,128)S(1)} %convolution_add_fusion.2, bf16[512,640]{1,0:T(8,128)(2,1)S(1)} %collective-permute-done.2, f32[256,512]{1,0:T(8,128)S(1)} %fusion.81, bf16[256,640]{1,0:T(8,128)(2,1)S(1)} %get-tuple-element.8, bf16[640,512]{1,0:T(8,128)(2,1)S(1)} %collective-permute-done.1), kind=kOutput, calls=%fused_computation.3 | convolution fusion | flops 337182720 | bytes 4128768 | tf_op jit(solution)/shard_map/dot_general | solution.py:27
  67.6 0.0 collective-permute-done.6
  67.6 1.4 %fusion.83 = f32[256,512]{1,0:T(8,128)S(1)} fusion(bf16[256,640]{1,0:T(8,128)(2,1)S(1)} %get-tuple-element.8, bf16[640,512]{1,0:T(8,128)(2,1)} %collective-permute-done.6), kind=kOutput, calls=%fused_computation.85 | convolution fusion | flops 167772160 | bytes 1507328 | tf_op jit(solution)/shard_map/dot_general | solution.py:27
  69.1 0.0 collective-permute-done.8
  69.1 2.7 %fusion.1 = bf16[256,640]{1,0:T(8,128)(2,1)} fusion(f32[256,640]{1,0:T(8,128)S(1)} %fusion, bf16[512,640]{1,0:T(8,128)(2,1)} %collective-permute-done.8, f32[256,512]{1,0:T(8,128)S(1)} %fusion.83, bf16[256,640]{1,0:T(8,128)(2,1)S(1)} %get-tuple-element.8, bf16[640,512]{1,0:T(8,128)(2,1)} %collective-permute-done.7), kind=kOutput, calls=%fused_computation.5 | convolution fusion | flops 337182720 | bytes 3145728 | tf_op jit(solution)/shard_map/dot_general | solution.py:27
  (10 shorter events, 0.0 us)
Async XLA Ops:
  0.6 58.4 %collective-permute-start.3 = (bf16[640,512]{1,0:T(8,128)(2,1)}, bf16[640,512]{1,0:T(8,128)(2,1)}, u32[]{:S(2)}, u32[]{:S(2)}) collective-permute-start(bf16[640,512]{1,0:T(8,128)(2,1)} %param.23), channel_id=1, source_target_pairs={{0,2},{1,3},{2,0},{3,1},{4,6},{5,7},{6,4},{7,5}} | collective-permute-start | bytes 1966088 | tf_op jit(solution)/shard_map/ppermute | solution.py:244
  4.0 59.9 %collective-permute-start = (bf16[640,512]{1,0:T(8,128)(2,1)}, bf16[640,512]{1,0:T(8,128)(2,1)}, u32[]{:S(2)}, u32[]{:S(2)}) collective-permute-start(bf16[640,512]{1,0:T(8,128)(2,1)} %param.23), channel_id=1, source_target_pairs={{0,1},{1,0},{2,3},{3,2},{4,5},{5,4},{6,7},{7,6}} | collective-permute-start | bytes 1966088 | tf_op jit(solution)/shard_map/ppermute | solution.py:245
  4.0 56.5 %collective-permute-start.4 = (bf16[640,512]{1,0:T(8,128)(2,1)}, bf16[640,512]{1,0:T(8,128)(2,1)}, u32[]{:S(2)}, u32[]{:S(2)}) collective-permute-start(bf16[640,512]{1,0:T(8,128)(2,1)} %param.24), channel_id=1, source_target_pairs={{0,2},{1,3},{2,0},{3,1},{4,6},{5,7},{6,4},{7,5}} | collective-permute-start | bytes 1966088 | tf_op jit(solution)/shard_map/ppermute | solution.py:244
  4.1 61.8 %collective-permute-start.1 = (bf16[640,512]{1,0:T(8,128)(2,1)}, bf16[640,512]{1,0:T(8,128)(2,1)S(1)}, u32[]{:S(2)}, u32[]{:S(2)}) collective-permute-start(bf16[640,512]{1,0:T(8,128)(2,1)} %param.24), channel_id=1, source_target_pairs={{0,1},{1,0},{2,3},{3,2},{4,5},{5,4},{6,7},{7,6}} | collective-permute-start | bytes 1966088 | tf_op jit(solution)/shard_map/ppermute | solution.py:245
  4.5 56.5 %collective-permute-start.5 = (bf16[512,640]{1,0:T(8,128)(2,1)}, bf16[512,640]{1,0:T(8,128)(2,1)}, u32[]{:S(2)}, u32[]{:S(2)}) collective-permute-start(bf16[512,640]{1,0:T(8,128)(2,1)} %param.25), channel_id=1, source_target_pairs={{0,2},{1,3},{2,0},{3,1},{4,6},{5,7},{6,4},{7,5}} | collective-permute-start | bytes 1966088 | tf_op jit(solution)/shard_map/ppermute | solution.py:244
  7.6 1.0 %copy-start = (bf16[256,640]{1,0:T(8,128)(2,1)S(1)}, bf16[256,640]{1,0:T(8,128)(2,1)}, u32[]{:S(2)}) copy-start(bf16[256,640]{1,0:T(8,128)(2,1)} %x_ref.1) | copy-start | bytes 983044
  8.6 1.0 %copy-start.1 = (bf16[640,256]{1,0:T(8,128)(2,1)S(1)}, bf16[640,256]{1,0:T(8,128)(2,1)}, u32[]{:S(2)}) copy-start(bf16[640,256]{1,0:T(8,128)(2,1)} %wk_ref.1) | copy-start | bytes 983044
  9.6 1.0 %copy-start.2 = (bf16[640,256]{1,0:T(8,128)(2,1)S(1)}, bf16[640,256]{1,0:T(8,128)(2,1)}, u32[]{:S(2)}) copy-start(bf16[640,256]{1,0:T(8,128)(2,1)} %wv_ref.1) | copy-start | bytes 983044
  10.6 0.7 copy-start.3
  11.2 45.6 %copy-start.4 = (bf16[640,512]{1,0:T(8,128)(2,1)S(1)}, bf16[640,512]{1,0:T(8,128)(2,1)}, u32[]{:S(2)}) copy-start(bf16[640,512]{1,0:T(8,128)(2,1)} %param.23) | copy-start | bytes 1966084
  11.2 46.0 %copy-start.5 = (bf16[640,512]{1,0:T(8,128)(2,1)S(1)}, bf16[640,512]{1,0:T(8,128)(2,1)}, u32[]{:S(2)}) copy-start(bf16[640,512]{1,0:T(8,128)(2,1)} %param.24) | copy-start | bytes 1966084
  59.0 6.8 %collective-permute-start.2 = (bf16[512,640]{1,0:T(8,128)(2,1)}, bf16[512,640]{1,0:T(8,128)(2,1)S(1)}, u32[]{:S(2)}, u32[]{:S(2)}) collective-permute-start(bf16[512,640]{1,0:T(8,128)(2,1)} %param.25), channel_id=1, source_target_pairs={{0,1},{1,0},{2,3},{3,2},{4,5},{5,4},{6,7},{7,6}} | collective-permute-start | bytes 1966088 | tf_op jit(solution)/shard_map/ppermute | solution.py:245
  60.5 7.1 %collective-permute-start.6 = (bf16[640,512]{1,0:T(8,128)(2,1)}, bf16[640,512]{1,0:T(8,128)(2,1)}, u32[]{:S(2)}, u32[]{:S(2)}) collective-permute-start(bf16[640,512]{1,0:T(8,128)(2,1)} %collective-permute-done.3), channel_id=1, source_target_pairs={{0,1},{1,0},{2,3},{3,2},{4,5},{5,4},{6,7},{7,6}} | collective-permute-start | bytes 1966088 | tf_op jit(solution)/shard_map/ppermute | solution.py:247
  61.0 8.1 %collective-permute-start.7 = (bf16[640,512]{1,0:T(8,128)(2,1)}, bf16[640,512]{1,0:T(8,128)(2,1)}, u32[]{:S(2)}, u32[]{:S(2)}) collective-permute-start(bf16[640,512]{1,0:T(8,128)(2,1)} %collective-permute-done.4), channel_id=1, source_target_pairs={{0,1},{1,0},{2,3},{3,2},{4,5},{5,4},{6,7},{7,6}} | collective-permute-start | bytes 1966088 | tf_op jit(solution)/shard_map/ppermute | solution.py:247
  63.9 5.2 %collective-permute-start.8 = (bf16[512,640]{1,0:T(8,128)(2,1)}, bf16[512,640]{1,0:T(8,128)(2,1)}, u32[]{:S(2)}, u32[]{:S(2)}) collective-permute-start(bf16[512,640]{1,0:T(8,128)(2,1)} %collective-permute-done.5), channel_id=1, source_target_pairs={{0,1},{1,0},{2,3},{3,2},{4,5},{5,4},{6,7},{7,6}} | collective-permute-start | bytes 1966088 | tf_op jit(solution)/shard_map/ppermute | solution.py:247

commit v2 on v0

v2 whole, which is shorter than its diff:
```python
import functools
import math

import jax
import jax.numpy as jnp
from jax import lax
from jax.experimental import pallas as pl
from jax.experimental.pallas import tpu as pltpu
from jax.sharding import PartitionSpec as P

HEADS = 4
HEAD_DIM = 256
HALF = HEAD_DIM // 2
GROUP = 16
RING = 4
TABLE = 512


def VIA_XLU(b):
    return b % 2 == 0

BLOCK = 128
STACK = HEADS * GROUP
F32 = jnp.float32
BF16 = jnp.bfloat16


def dot(a, b):
    return jnp.dot(a, b, preferred_element_type=F32)


def dot_t(a, b):
    return lax.dot_general(a, b, (((1,), (1,)), ((), ())), preferred_element_type=F32)


def rms_scale(wide_vals, gain):
    inv_rms = lax.rsqrt(jnp.mean(wide_vals * wide_vals, axis=-1, keepdims=True) + 1e-6)
    return (wide_vals * inv_rms * (1.0 + gain)).astype(BF16)


def tile_heads(t):
    return jnp.concatenate([t] * HEADS, axis=0)


def attend_groups(parity, count, cache_size, table, k_hbm, v_hbm, kbuf, vbuf, ksem, vsem, s_buf, p_buf, pn_buf,
                  load_q, load_k, load_v, load_len, store, prepare):
    max_nb = cache_size // BLOCK

    def first_row(p):
        return (2 * p + parity) * GROUP

    def slot_row(p, b):
        return pl.multiple_of(((p & (RING - 1)) * GROUP + b) * cache_size, cache_size)

    def issue(hbm, buf, sems, p):
        for b in range(GROUP):
            src = pl.multiple_of(table[0, first_row(p) + b], cache_size)
            size = pl.multiple_of(table[1, first_row(p) + b], 16)
            pltpu.make_async_copy(hbm.at[pl.ds(src, size)], buf.at[pl.ds(slot_row(p, b), size)],
                                  sems.at[p & (RING - 1)]).start()

    def wait(hbm, buf, sems, p):
        n = pl.multiple_of(table[3, first_row(p)], 16)
        pltpu.make_async_copy(hbm.at[pl.ds(0, n)], buf.at[pl.ds(0, n)], sems.at[p & (RING - 1)]).wait()

    def blocks(p):
        return (table[1, first_row(p)] + (BLOCK - 1)) >> 7

    zeros = jnp.zeros((BLOCK, HEAD_DIM), BF16)

    def fill(p, c):
        upto = jnp.where(p < 1, max_nb, blocks(jnp.maximum(p - 1, 0)))
        for b in range(GROUP):
            base = slot_row(p, b)
            own = (table[1, first_row(p) + b] + (BLOCK - 1)) >> 7

            def clear(t, c):
                at = pl.multiple_of(base + t * BLOCK, BLOCK)
                kbuf[pl.ds(at, BLOCK), :] = zeros
                vbuf[pl.ds(at, BLOCK), :] = zeros
                return c
            lax.fori_loop(own - 1, upto, clear, 0)
        issue(k_hbm, kbuf, ksem, p)
        issue(v_hbm, vbuf, vsem, p)
        return c
    lax.fori_loop(0, RING, fill, 0)

    prepare()

    def scores(p, nb):
        q = load_q(2 * p + parity)
        member = lax.broadcasted_iota(jnp.int32, (STACK, HEAD_DIM), 0) % GROUP
        out = None
        for b in range(GROUP):
            k_b = kbuf[pl.ds(slot_row(p, b), nb * BLOCK), :]
            q_b = jnp.where(member == b, q, jnp.zeros_like(q))
            if VIA_XLU(b):
                k_t = k_b.T
                lane = lax.broadcasted_iota(jnp.int32, k_t.shape, 1)
                part = dot(q_b, jnp.where(lane < table[1, first_row(p) + b], k_t, jnp.zeros_like(k_t)))
            else:
                part = dot_t(q_b, k_b)
            out = part if out is None else out + part
        return out

    def softmax(p, s):
        width = s.shape[1]
        start = pl.multiple_of(first_row(p), GROUP)
        lens = tile_heads(load_len(start))[:, :1]
        valid = lax.broadcasted_iota(jnp.int32, (STACK, width), 1).astype(F32) < lens
        s_new = jnp.sum(load_q(2 * p + parity).astype(F32) * tile_heads(load_k(start)), axis=-1, keepdims=True)
        s = jnp.where(valid, s, -jnp.inf)
        peak = jnp.maximum(jnp.max(s, axis=-1, keepdims=True), s_new)
        w = jnp.exp(s - peak)
        w_new = jnp.exp(s_new - peak)
        inv = 1.0 / (jnp.sum(w, axis=-1, keepdims=True) + w_new)
        prob_new = (w_new * inv).astype(BF16).astype(F32)
        return (w * inv).astype(BF16), jnp.broadcast_to(prob_new, (STACK, 128))

    def values(p, prob, prob_new):
        width = prob.shape[1]
        start = pl.multiple_of(first_row(p), GROUP)
        member = lax.broadcasted_iota(jnp.int32, (STACK, width), 0) % GROUP
        out = None
        for b in range(GROUP):
            part = dot(jnp.where(member == b, prob, jnp.zeros_like(prob)), vbuf[pl.ds(slot_row(p, b), width), :])
            out = part if out is None else out + part
        store(p, out + prob_new[:, :1] * tile_heads(load_v(start)))

    wait(k_hbm, kbuf, ksem, 0)
    s_buf[...] = scores(0, max_nb)
    issue(k_hbm, kbuf, ksem, RING)

    def step(p, c):
        nb_p = blocks(p)
        wait(k_hbm, kbuf, ksem, p + 1)
        for nb in range(1, max_nb + 1):
            @pl.when(nb_p == nb)
            def _():
                width = nb * BLOCK
                nxt = scores(p + 1, nb)
                prob, prob_new = softmax(p, s_buf[:, :width])
                s_buf[:, :width] = nxt
                p_buf[:, :width] = prob
                pn_buf[...] = prob_new
        issue(k_hbm, kbuf, ksem, p + 1 + RING)
        wait(v_hbm, vbuf, vsem, p)
        for nb in range(1, max_nb + 1):
            @pl.when(nb_p == nb)
            def _():
                width = nb * BLOCK
                values(p, p_buf[:, :width], pn_buf[...])
        issue(v_hbm, vbuf, vsem, p + RING)
        return c
    lax.fori_loop(0, count, step, 0)


def first_kernel(rows, cache_size, x_in, len_in, na_ref, wq, wk, wv, k_hbm, v_hbm,
                 knew_ref, vnew_ref, table_out, q_out, ks_out, vs_out, len_out, o_out,
                 kbuf, vbuf, s_buf, p_buf, pn_buf, table, ksem, vsem, tsem):
    groups = rows // GROUP

    len_row = len_in[...].astype(F32)
    lane_id = lax.broadcasted_iota(jnp.int32, (1, rows), 1).astype(F32)
    key_row = len_row * rows + (rows - 1 - lane_id)
    key_col = jnp.broadcast_to(key_row, (128, rows)).T[:, :1]
    len_col = jnp.broadcast_to(len_row, (128, rows)).T[:, :1]
    sub_id = lax.broadcasted_iota(jnp.int32, (rows, rows), 0).astype(F32)
    lane_sq = lax.broadcasted_iota(jnp.int32, (rows, rows), 1).astype(F32)
    rank_row = jnp.sum((key_col > key_row).astype(F32), axis=0, keepdims=True)
    rank_col = jnp.sum((key_row > key_col).astype(F32), axis=1, keepdims=True)
    to_natural = rank_col == lane_sq
    perm_row = jnp.sum(jnp.where(to_natural, sub_id, 0.0), axis=0, keepdims=True).astype(jnp.int32)
    slen_row = jnp.sum(jnp.where(to_natural, len_col, 0.0), axis=0, keepdims=True).astype(jnp.int32)
    table_out[...] = jnp.zeros(table_out.shape, jnp.int32)
    size_row = jnp.maximum((slen_row + 15) & -16, 16)
    group_row = size_row
    for shift in (1, 2, 4, 8):
        group_row = group_row + pltpu.roll(group_row, rows - shift, 1)
    table_out[0:1, :rows] = perm_row * cache_size
    table_out[1:2, :rows] = size_row
    table_out[2:3, :rows] = perm_row
    table_out[3:4, :rows] = group_row
    table_copy = pltpu.make_async_copy(table_out, table, tsem)
    table_copy.start()
    table_copy.wait()

    def prepare():
        to_sorted = rank_row == sub_id
        slen_col = jnp.sum(jnp.where(to_sorted, len_row, 0.0), axis=1, keepdims=True)
        len_out[:rows, :] = jnp.broadcast_to(slen_col, (rows, 128))
        xn = rms_scale(x_in[...].astype(F32), na_ref[...].astype(F32))
        lane = lax.broadcasted_iota(jnp.int32, (1, HALF), 1).astype(F32)
        angles = len_col * jnp.exp(lane * (-2.0 / HEAD_DIM * math.log(10000.0)))
        cos_t, sin_t = jnp.cos(angles), jnp.sin(angles)

        def rotary(val):
            first, second = val[:, :HALF], val[:, HALF:]
            return jnp.concatenate([first * cos_t - second * sin_t, second * cos_t + first * sin_t], axis=-1)

        pick = to_sorted.astype(BF16)
        k_bf = rotary(dot(xn, wk[...])).astype(BF16)
        v_bf = dot(xn, wv[...]).astype(BF16)
        knew_ref[...] = k_bf
        vnew_ref[...] = v_bf
        ks_out[:rows, :] = dot(pick, k_bf)
        vs_out[:rows, :] = dot(pick, v_bf)
        for h in range(HEADS):
            q_h = (rotary(dot(xn, wq[:, h * HEAD_DIM:(h + 1) * HEAD_DIM])) * HEAD_DIM ** -0.5).astype(BF16)
            q_out[0:groups, h * GROUP:(h + 1) * GROUP, :] = dot(pick, q_h).reshape(groups, GROUP, HEAD_DIM)
        for g in range(groups, groups + 4):
            q_out[g] = jnp.zeros((STACK, HEAD_DIM), F32)
        pad = 2 * GROUP
        ks_out[rows:, :] = jnp.zeros((pad, HEAD_DIM), F32)
        vs_out[rows:, :] = jnp.zeros((pad, HEAD_DIM), F32)
        len_out[rows:, :] = jnp.zeros((pad, 128), F32)

    def store(p, out):
        for h in range(HEADS):
            o_out[pl.ds(pl.multiple_of(p * GROUP, GROUP), GROUP), h * HEAD_DIM:(h + 1) * HEAD_DIM] = out[h * GROUP:(h + 1) * GROUP]

    attend_groups(0, groups // 2, cache_size, table, k_hbm, v_hbm, kbuf, vbuf, ksem, vsem, s_buf, p_buf, pn_buf,
                  lambda g: q_out[g].astype(BF16), lambda s: ks_out[pl.ds(s, GROUP), :], lambda s: vs_out[pl.ds(s, GROUP), :],
                  lambda s: len_out[pl.ds(s, GROUP), :], store, prepare)


def second_kernel(rows, cache_size, table, x_in, q_in, ks_in, vs_in, len_in, o_even, nm_ref, tab_in, wo, k_hbm, v_hbm,
                  x1_ref, xn2_ref,
                  kbuf, vbuf, o_odd, s_buf, p_buf, pn_buf, ksem, vsem):
    groups = rows // GROUP

    def prepare():
        pass

    def store(p, out):
        for h in range(HEADS):
            o_odd[pl.ds(pl.multiple_of(p * GROUP, GROUP), GROUP), h * HEAD_DIM:(h + 1) * HEAD_DIM] = out[h * GROUP:(h + 1) * GROUP]

    attend_groups(1, groups // 2, cache_size, table, k_hbm, v_hbm, kbuf, vbuf, ksem, vsem, s_buf, p_buf, pn_buf,
                  lambda g: q_in[g].astype(BF16), lambda s: ks_in[pl.ds(s, GROUP), :], lambda s: vs_in[pl.ds(s, GROUP), :],
                  lambda s: len_in[pl.ds(s, GROUP), :], store, prepare)

    perm = tab_in[2:3, :rows]
    natural = lax.broadcasted_iota(jnp.int32, (rows, rows), 0)
    back = (natural == perm).astype(BF16)
    o_all = jnp.concatenate([o_even[...].reshape(groups // 2, GROUP, HEADS * HEAD_DIM),
                             o_odd[...].reshape(groups // 2, GROUP, HEADS * HEAD_DIM)], axis=1).reshape(rows, HEADS * HEAD_DIM).astype(BF16)
    mixed = dot(dot(back, o_all).astype(BF16), wo[...])
    x1 = x_in[...].astype(F32) + mixed
    x1_ref[...] = x1
    xn2_ref[...] = rms_scale(x1, nm_ref[...].astype(F32))


def shape(dims, dtype):
    return jax.ShapeDtypeStruct(dims, dtype)


VMEM_SPEC = pl.BlockSpec(memory_space=pltpu.VMEM)
SMEM_SPEC = pl.BlockSpec(memory_space=pltpu.SMEM)
HBM_SPEC = pl.BlockSpec(memory_space=pl.ANY)


def ring_scratch(cache_size):
    return [pltpu.VMEM((RING * GROUP * cache_size, HEAD_DIM), BF16)] * 2


def attention_first(hidden_in, k_cache, v_cache, cache_len, norm_attn, w_q, w_k, w_v):
    rows, d_model = hidden_in.shape
    cache_size = k_cache.shape[1]
    groups = rows // GROUP
    width = HEADS * HEAD_DIM
    k_flat = k_cache.reshape(rows * cache_size, HEAD_DIM)
    v_flat = v_cache.reshape(rows * cache_size, HEAD_DIM)
    params = pltpu.CompilerParams(vmem_limit_bytes=44 * 1024 * 1024)
    cost = pl.CostEstimate(flops=10 ** 10, bytes_accessed=4 * 10 ** 7, transcendentals=10 ** 6)
    sems = [pltpu.SemaphoreType.DMA((RING,)), pltpu.SemaphoreType.DMA((RING,))]
    return pl.pallas_call(
        functools.partial(first_kernel, rows, cache_size),
        out_shape=(shape((rows, HEAD_DIM), BF16), shape((rows, HEAD_DIM), BF16), shape((8, TABLE), jnp.int32),
                   shape((groups + 4, STACK, HEAD_DIM), F32), shape((rows + 2 * GROUP, HEAD_DIM), F32), shape((rows + 2 * GROUP, HEAD_DIM), F32),
                   shape((rows + 2 * GROUP, 128), F32), shape((rows // 2, width), F32)),
        in_specs=[VMEM_SPEC] * 6 + [HBM_SPEC] * 2,
        out_specs=(VMEM_SPEC,) * 8,
        scratch_shapes=ring_scratch(cache_size) + [
            pltpu.VMEM((STACK, cache_size), F32),
            pltpu.VMEM((STACK, cache_size), BF16),
            pltpu.VMEM((STACK, 128), F32),
            pltpu.SMEM((8, TABLE), jnp.int32),
        ] + sems + [pltpu.SemaphoreType.DMA],
        compiler_params=params,
        cost_estimate=cost,
        name='attention_first',
    )(hidden_in, cache_len.reshape(1, rows), norm_attn.reshape(1, d_model), w_q, w_k, w_v, k_flat, v_flat)


def attention_second(hidden_in, k_cache, v_cache, norm_mlp, w_o, table, q_s, k_s, v_s, len_s, o_even):
    rows, d_model = hidden_in.shape
    cache_size = k_cache.shape[1]
    groups = rows // GROUP
    width = HEADS * HEAD_DIM
    k_flat = k_cache.reshape(rows * cache_size, HEAD_DIM)
    v_flat = v_cache.reshape(rows * cache_size, HEAD_DIM)
    params = pltpu.CompilerParams(vmem_limit_bytes=44 * 1024 * 1024)
    cost = pl.CostEstimate(flops=10 ** 10, bytes_accessed=4 * 10 ** 7, transcendentals=10 ** 6)
    sems = [pltpu.SemaphoreType.DMA((RING,)), pltpu.SemaphoreType.DMA((RING,))]
    return pl.pallas_call(
        functools.partial(second_kernel, rows, cache_size),
        out_shape=(shape((rows, d_model), F32), shape((rows, d_model), BF16)),
        in_specs=[SMEM_SPEC] + [VMEM_SPEC] * 9 + [HBM_SPEC] * 2,
        out_specs=(VMEM_SPEC,) * 2,
        scratch_shapes=ring_scratch(cache_size) + [
            pltpu.VMEM((rows // 2, width), F32),
            pltpu.VMEM((STACK, cache_size), F32),
            pltpu.VMEM((STACK, cache_size), BF16),
            pltpu.VMEM((STACK, 128), F32),
        ] + sems,
        compiler_params=params,
        cost_estimate=cost,
        name='attention_second',
    )(table, hidden_in, q_s, k_s, v_s, len_s, o_even, norm_mlp.reshape(1, d_model), table, w_o, k_flat, v_flat)


def attention(hidden_in, k_cache, v_cache, cache_len, norm_attn, norm_mlp, w_q, w_k, w_v, w_o):
    k_new, v_new, *state = attention_first(hidden_in, k_cache, v_cache, cache_len, norm_attn, w_q, w_k, w_v)
    x1, xn2 = attention_second(hidden_in, k_cache, v_cache, norm_mlp, w_o, *state)
    return x1, xn2, k_new, v_new


def gelu(x):
    return 0.5 * x * (1.0 + jnp.tanh(math.sqrt(2.0 / math.pi) * (x + 0.044715 * (x * x * x))))


def mlp_kernel(shards, last, swap_at, *refs):
    x1_ref, xn_ref = refs[0], refs[1]
    weights = refs[2:2 + 3 * shards]
    out_ref = refs[2 + 3 * shards]
    straight = lax.axis_index('dp') == 0
    xn = xn_ref[...]
    total = x1_ref[...]
    for i in range(shards):
        first, second, down = weights[3 * i:3 * i + 3]
        parts = []
        for half in range(2):
            cols = slice(half * 256, half * 256 + 256)
            gate_act = dot(xn, first[:, cols])
            up_act = dot(xn, second[:, cols])
            if i == swap_at:
                gate_act, up_act = jnp.where(straight, gate_act, up_act), jnp.where(straight, up_act, gate_act)
            parts.append((gelu(gate_act) * up_act).astype(BF16))
        total = total + dot(jnp.concatenate(parts, axis=1), down[...])
    out_ref[...] = total.astype(out_ref.dtype)


def mlp(x1, xn, shards, last, swap_at):
    rows, d_model = xn.shape
    units = shards[0][0].shape[1]
    n = len(shards)
    return pl.pallas_call(
        functools.partial(mlp_kernel, n, last, swap_at),
        out_shape=shape((rows, d_model), BF16 if last else F32),
        in_specs=[VMEM_SPEC] * (2 + 3 * n),
        out_specs=VMEM_SPEC,
        compiler_params=pltpu.CompilerParams(vmem_limit_bytes=24 * 1024 * 1024),
        cost_estimate=pl.CostEstimate(flops=6 * rows * d_model * units * n, bytes_accessed=6 * d_model * units * n, transcendentals=rows * units * n),
        name='mlp',
    )(x1, xn, *[w for triple in shards for w in triple])


CORE = [(0, 1), (1, 0), (2, 3), (3, 2)]
ACROSS = [(0, 2), (1, 3), (2, 0), (3, 1)]
ROWS = [(0, 1), (1, 0)]


def solution(mesh):
    row_spec = P(('dp', 'tp'), None)
    cache_spec = P(('dp', 'tp'), None, None)
    full_vec = P(None)
    full_mat = P(None, None)

    def per_device(hidden_in, k_cache, v_cache, cache_len, norm_attn, norm_mlp, w_q, w_k, w_v, w_o, w_gate, w_up, w_down):
        half = jnp.where(lax.axis_index('dp') == 0, w_gate, w_up)
        half_far = lax.ppermute(half, 'tp', ACROSS)
        near = tuple(lax.ppermute(w, 'tp', CORE) for w in (w_gate, w_up, w_down))
        k_new, v_new, *state = attention_first(hidden_in, k_cache, v_cache, cache_len, norm_attn, w_q, w_k, w_v)
        half_far, down_own, state = lax.optimization_barrier((half_far, w_down, state))
        other_far = lax.ppermute(half_far, 'dp', ROWS)
        down_far = lax.ppermute(down_own, 'tp', ACROSS)
        half_diag = lax.ppermute(half_far, 'tp', CORE)
        x_mid, xn_mid = attention_second(hidden_in, k_cache, v_cache, norm_mlp, w_o, *state)
        other_far, down_far, x_mid, xn_mid = lax.optimization_barrier((other_far, down_far, x_mid, xn_mid))
        other_diag = lax.ppermute(other_far, 'tp', CORE)
        down_diag = lax.ppermute(down_far, 'tp', CORE)
        part = mlp(x_mid, xn_mid, ((w_gate, w_up, w_down), near, (half_far, other_far, down_far)), False, 2)
        out = mlp(part, xn_mid, ((half_diag, other_diag, down_diag),), True, 0)
        return out, k_new, v_new

    return jax.shard_map(
        per_device,
        mesh=mesh,
        in_specs=(row_spec, cache_spec, cache_spec, P(('dp', 'tp')), full_vec, full_vec,
                  full_mat, full_mat, full_mat, full_mat, P(None, 'tp'), P(None, 'tp'), P('tp', None)),
        out_specs=(row_spec, row_spec, row_spec),
        check_vma=False,
    )
```

time: 143 us -> 55.4 us (0.39)
  matrix products: 65.3 us -> 0 us
  Pallas kernels: 0 us -> 44.8 us
  waiting for transfers between devices: 45.2 us -> 1.11 us
  between operations: 14.2 us -> 0.82 us
  other arithmetic: 12 us -> 1.16 us
  starting transfers between devices: 0.26 us -> 6.33 us
  local copies, waits for them, and re-layouts: 5.66 us -> 1.02 us
    dot_general x9 -> x0, matrix products: 65.3 us -> none  [the longest x1 25.6 us: attend(): jnp.einsum('bhd,btd->bht', q_rot, k_cache, preferred_element_type=jnp.flo...]
    pallas_call x0 -> x4, Pallas kernels: none -> 44.8 us  [the longest x1 21.5 us: attention_first(): pl.pallas_call(functools.partial(first_kernel, rows, cache_size), out_sha...]
    reduce_scatter x1 -> x0, waiting for transfers between devices: 27.2 us -> none  [per_device(): down_sum = lax.psum_scatter(part_sum, 'tp', scatter_dimension=0, tiled=True)]
    all_gather x1 -> x0, waiting for transfers between devices: 17.9 us -> none  [per_device(): group_rows = lax.all_gather(xn_mid, 'tp', axis=0, tiled=True)]
    ppermute x0 -> x9, starting transfers between devices: none -> 6.33 us  [the longest x1 3.02 us: per_device(): half_far = lax.ppermute(half, 'tp', ACROSS)]
    convert_element_type x5 -> x0, other arithmetic: 4.57 us -> none  [the longest x1 1.87 us: per_device(): return ((x_mid + down_sum).astype(jnp.bfloat16), k_new, v_new)]
    reduce_sum x2 -> x0, other arithmetic: 2.72 us -> none  [the longest x1 1.61 us: attend(): weight_sum = jnp.sum(hist_weight, axis=-1) + new_weight]
    unnamed x16 -> x22, local copies, waits for them, and re-layouts: 2.8 us -> 1.01 us
  transfers between devices with their start and end apart: 2 -> 9, of which waited for: 2 -> 2; matrix products, arithmetic and copies ran while one was open for 1% -> 2% of each run, Pallas kernels for 0% -> 78%
where the time goes in v2:
time: 55.4 us; the launch traced here: 55.2 us
  Pallas kernels  44.8 us (81%)
  starting transfers between devices  6.33 us (11%)
  other arithmetic  1.16 us (2%)
  waiting for transfers between devices  1.11 us (2%)
  local copies, waits for them, and re-layouts  1.02 us (2%)
  between operations  0.82 us (1%)
    pallas_call x1, Pallas kernels, attention_first(): pl.pallas_call(functools.partial(first_kernel, rows, cache_size), out_sha...  21.5 us
    pallas_call x1, Pallas kernels, attention_second(): pl.pallas_call(functools.partial(second_kernel, rows, cache_size), out_sh...  19.7 us
    pallas_call x2, Pallas kernels, mlp(): pl.pallas_call(functools.partial(mlp_kernel, n, last, swap_at), out_shape...  3.66 us
    ppermute x1, starting transfers between devices, per_device(): half_far = lax.ppermute(half, 'tp', ACROSS)  3.02 us
    ppermute x1, starting transfers between devices, per_device(): down_far = lax.ppermute(down_own, 'tp', ACROSS)  1.39 us
    select_n x1, other arithmetic, per_device(): half = jnp.where(lax.axis_index('dp') == 0, w_gate, w_up)  1.16 us
  transfers between devices with their start and end apart: 9, of which 2 were waited for; matrix products, arithmetic and copies ran while one was open for 2% of the time, Pallas kernels for 78%

profile of v2, /device:TPU:0, one launch (start us, length us, event | category | flops | bytes accessed | tf_op | source)
XLA Modules:
  0.0 55.2 jit_solution(9008569570647921010)
XLA Ops:
  0.6 0.0 copy-start.9
  0.6 0.0 copy-start.10
  0.7 0.9 %collective-permute-start.3 = (bf16[640,512]{1,0:T(8,128)(2,1)}, bf16[640,512]{1,0:T(8,128)(2,1)S(1)}, u32[]{:S(2)}, u32[]{:S(2)}) collective-permute-start(bf16[640,512]{1,0:T(8,128)(2,1)} %refs_2_.1), channel_id=1, source_target_pairs={{0,1},{1,0},{2,3},{3,2},{4,5},{5,4},{6,7},{7,6}} | collective-permute-start | bytes 1966088 | tf_op jit(solution)/shard_map/ppermute | solution.py:383
  1.6 0.0 collective-permute-start.4
  1.6 1.2 %broadcast_select_fusion = bf16[640,512]{1,0:T(8,128)(2,1)S(1)} fusion(bf16[640,512]{1,0:T(8,128)(2,1)} %refs_2_.1, bf16[640,512]{1,0:T(8,128)(2,1)} %refs_3_.1, pred[]{:T(512)S(6)} %eq.3), kind=kLoop, calls=%fused_computation | loop fusion | flops 327680 | bytes 1966081 | tf_op jit(solution)/shard_map/jit(_where)/select_n | solution.py:381
  2.8 3.0 %collective-permute-start = (bf16[640,512]{1,0:T(8,128)(2,1)S(1)}, bf16[640,512]{1,0:T(8,128)(2,1)S(1)}, u32[]{:S(2)}, u32[]{:S(2)}) collective-permute-start(bf16[640,512]{1,0:T(8,128)(2,1)S(1)} %broadcast_select_fusion), channel_id=1, source_target_pairs={{0,2},{1,3},{2,0},{3,1},{4,6},{5,7},{6,4},{7,5}} | collective-permute-start | bytes 1966088 | tf_op jit(solution)/shard_map/ppermute | solution.py:382
  5.8 0.0 collective-permute-start.5
  5.8 0.0 copy-done.9
  5.8 0.0 copy-done.10
  5.9 0.0 copy-start.7
  5.9 1.0 %copy-done.7 = bf16[640,256]{1,0:T(8,128)(2,1)S(1)} copy-done((bf16[640,256]{1,0:T(8,128)(2,1)S(1)}, bf16[640,256]{1,0:T(8,128)(2,1)}, u32[]{:S(2)}) %copy-start.7) | copy-done | bytes 327704
  6.8 21.5 %attention_first.1 = (bf16[256,256]{1,0:T(8,128)(2,1)}, bf16[256,256]{1,0:T(8,128)(2,1)}, s32[8,512]{1,0:T(8,128)S(1)}, f32[20,64,256]{2,1,0:T(8,128)S(1)}, f32[...) custom-call(bf16[256,640]{1,0:T(8,128)(2,1)S(1)} %copy-done.3, ...), custom_call_target="tpu_custom_call" | custom-call | flops 10000000000 | bytes 40000000 | tf_op jit(solution)/shard_map/attention_first/pallas_call | solution.py:277
  28.3 0.0 collective-permute-done.refs_8_
  28.3 0.0 copy-start
  28.3 0.0 copy-start.1
  28.3 0.3 collective-permute-start.1
  28.6 0.0 copy-done.5
  28.6 1.4 %collective-permute-start.2 = (bf16[512,640]{1,0:T(8,128)(2,1)S(1)}, bf16[512,640]{1,0:T(8,128)(2,1)S(1)}, u32[]{:S(2)}, u32[]{:S(2)}) collective-permute-start(bf16[512,640]{1,0:T(8,128)(2,1)S(1)} %copy-done.5), channel_id=1, source_target_pairs={{0,2},{1,3},{2,0},{3,1},{4,6},{5,7},{6,4},{7,5}} | collective-permute-start | bytes 1966088 | tf_op jit(solution)/shard_map/ppermute | solution.py:387
  30.0 19.7 %attention_second.1 = (f32[256,640]{1,0:T(8,128)S(1)}, bf16[256,640]{1,0:T(8,128)(2,1)S(1)}) custom-call(s32[8,512]{1,0:T(8,128)S(1)} %get-tuple-element.33.table.tab_in, bf16[256,640]{1,0:T(8,128)(2,1)S(1)} %copy-done.3, f32[20,64,256]{2,1,0:T(8,128)S(1)} %get-tuple-element.34.q_in, f32[288,256]{1,0:T(8,128)S(1)} %get-tuple-element.35.ks_in, ...), custom_call_target="tpu_custom_call" | custom-call | flops 10000000000 | bytes 40000000 | tf_op jit(solution)/shard_map/attention_second/pallas_call | solution.py:306
  49.7 0.0 collective-permute-done.1.refs_9_
  49.7 0.2 collective-permute-start.6
  49.9 0.0 collective-permute-done.2.refs_10_
  49.9 0.3 collective-permute-start.7
  50.2 0.0 collective-permute-done.3.refs_5_
  50.2 0.2 collective-permute-start.8
  50.4 0.0 collective-permute-done.4.refs_6_
  50.4 0.0 collective-permute-done.5.refs_7_
  50.5 2.1 %mlp.2.refs_0_ = f32[256,640]{1,0:T(8,128)S(1)} custom-call(f32[256,640]{1,0:T(8,128)S(1)} %get-tuple-element.41.refs_0_, bf16[256,640]{1,0:T(8,128)(2,1)S(1)} %get-tuple-element.42.refs_1_, bf16[640,512]{1,0:T(8,128)(2,1)S(1)} %copy-done, bf16[640,512]{1,0:T(8,128)(2,1)S(1)} %copy-done.1, bf16[512,640]{1,0:T(8,128)(2,1)S(1)} %copy-done.5, ...), custom_call_target="tpu_custom_call" | custom-call | flops 1509949440 | bytes 5898240 | tf_op jit(solution)/shard_map/mlp/pallas_call | solution.py:358
  52.6 0.0 collective-permute-done.6.refs_2_
  52.6 0.2 collective-permute-done.7.refs_3_
  52.7 0.9 %collective-permute-done.8.refs_4_ = bf16[512,640]{1,0:T(8,128)(2,1)S(1)} collective-permute-done((bf16[512,640]{1,0:T(8,128)(2,1)S(1)}, bf16[512,640]{1,0:T(8,128)(2,1)S(1)}, u32[]{:S(2)}, u32[]{:S(2)}) %collective-permute-start.8) | collective-permute-done | bytes 655392 | tf_op jit(solution)/shard_map/ppermute | solution.py:392
  53.7 1.6 %mlp.3 = bf16[256,640]{1,0:T(8,128)(2,1)} custom-call(f32[256,640]{1,0:T(8,128)S(1)} %mlp.2.refs_0_, bf16[256,640]{1,0:T(8,128)(2,1)S(1)} %get-tuple-element.42.refs_1_, bf16[640,512]{1,0:T(8,128)(2,1)S(1)} %collective-permute-done.6.refs_2_, bf16[640,512]{1,0:T(8,128)(2,1)S(1)} %collective-permute-done.7.refs_3_, ...), custom_call_target="tpu_custom_call" | custom-call | flops 503316480 | bytes 1966080 | tf_op jit(solution)/shard_map/mlp/pallas_call | solution.py:358
  (15 shorter events, 0.0 us)
Async XLA Ops:
  0.6 5.2 %copy-start.9 = (bf16[640]{0:T(1024)(128)(2,1)S(1)}, bf16[640]{0:T(1024)(128)(2,1)}, u32[]{:S(2)}) copy-start(bf16[640]{0:T(1024)(128)(2,1)} %param.17) | copy-start | bytes 3844
  0.6 5.2 %copy-start.10 = (bf16[640]{0:T(1024)(128)(2,1)S(1)}, bf16[640]{0:T(1024)(128)(2,1)}, u32[]{:S(2)}) copy-start(bf16[640]{0:T(1024)(128)(2,1)} %param.18) | copy-start | bytes 3844
  0.7 5.2 %copy-start.8 = (s32[256]{0:T(256)S(1)}, s32[256]{0:T(256)}, u32[]{:S(2)}) copy-start(s32[256]{0:T(256)} %param.16) | copy-start | bytes 3076
  0.7 5.2 %copy-start.3 = (bf16[256,640]{1,0:T(8,128)(2,1)S(1)}, bf16[256,640]{1,0:T(8,128)(2,1)}, u32[]{:S(2)}) copy-start(bf16[256,640]{1,0:T(8,128)(2,1)} %x_in.3) | copy-start | bytes 983044
  0.7 5.2 %copy-start.2 = (bf16[640,1024]{1,0:T(8,128)(2,1)S(1)}, bf16[640,1024]{1,0:T(8,128)(2,1)}, u32[]{:S(2)}) copy-start(bf16[640,1024]{1,0:T(8,128)(2,1)} %wq.1) | copy-start | bytes 3932164
  0.7 5.2 %copy-start.6 = (bf16[640,256]{1,0:T(8,128)(2,1)S(1)}, bf16[640,256]{1,0:T(8,128)(2,1)}, u32[]{:S(2)}) copy-start(bf16[640,256]{1,0:T(8,128)(2,1)} %wk.1) | copy-start | bytes 983044
  0.7 49.5 %collective-permute-start.3 = (bf16[640,512]{1,0:T(8,128)(2,1)}, bf16[640,512]{1,0:T(8,128)(2,1)S(1)}, u32[]{:S(2)}, u32[]{:S(2)}) collective-permute-start(bf16[640,512]{1,0:T(8,128)(2,1)} %refs_2_.1), channel_id=1, source_target_pairs={{0,1},{1,0},{2,3},{3,2},{4,5},{5,4},{6,7},{7,6}} | collective-permute-start | bytes 1966088 | tf_op jit(solution)/shard_map/ppermute | solution.py:383
  1.6 48.9 %collective-permute-start.4 = (bf16[640,512]{1,0:T(8,128)(2,1)}, bf16[640,512]{1,0:T(8,128)(2,1)S(1)}, u32[]{:S(2)}, u32[]{:S(2)}) collective-permute-start(bf16[640,512]{1,0:T(8,128)(2,1)} %refs_3_.1), channel_id=1, source_target_pairs={{0,1},{1,0},{2,3},{3,2},{4,5},{5,4},{6,7},{7,6}} | collective-permute-start | bytes 1966088 | tf_op jit(solution)/shard_map/ppermute | solution.py:383
  2.8 25.5 %collective-permute-start = (bf16[640,512]{1,0:T(8,128)(2,1)S(1)}, bf16[640,512]{1,0:T(8,128)(2,1)S(1)}, u32[]{:S(2)}, u32[]{:S(2)}) collective-permute-start(bf16[640,512]{1,0:T(8,128)(2,1)S(1)} %broadcast_select_fusion), channel_id=1, source_target_pairs={{0,2},{1,3},{2,0},{3,1},{4,6},{5,7},{6,4},{7,5}} | collective-permute-start | bytes 1966088 | tf_op jit(solution)/shard_map/ppermute | solution.py:382
  5.8 44.6 %collective-permute-start.5 = (bf16[512,640]{1,0:T(8,128)(2,1)}, bf16[512,640]{1,0:T(8,128)(2,1)S(1)}, u32[]{:S(2)}, u32[]{:S(2)}) collective-permute-start(bf16[512,640]{1,0:T(8,128)(2,1)} %refs_4_.1), channel_id=1, source_target_pairs={{0,1},{1,0},{2,3},{3,2},{4,5},{5,4},{6,7},{7,6}} | collective-permute-start | bytes 1966088 | tf_op jit(solution)/shard_map/ppermute | solution.py:383
  5.9 1.0 %copy-start.7 = (bf16[640,256]{1,0:T(8,128)(2,1)S(1)}, bf16[640,256]{1,0:T(8,128)(2,1)}, u32[]{:S(2)}) copy-start(bf16[640,256]{1,0:T(8,128)(2,1)} %wv.1) | copy-start | bytes 983044
  6.8 21.8 %copy-start.5 = (bf16[512,640]{1,0:T(8,128)(2,1)S(1)}, bf16[512,640]{1,0:T(8,128)(2,1)}, u32[]{:S(2)}) copy-start(bf16[512,640]{1,0:T(8,128)(2,1)} %refs_4_.1) | copy-start | bytes 1966084
  6.8 23.2 %copy-start.4 = (bf16[1024,640]{1,0:T(8,128)(2,1)S(1)}, bf16[1024,640]{1,0:T(8,128)(2,1)}, u32[]{:S(2)}) copy-start(bf16[1024,640]{1,0:T(8,128)(2,1)} %wo.1) | copy-start | bytes 3932164
  28.3 22.1 %copy-start = (bf16[640,512]{1,0:T(8,128)(2,1)S(1)}, bf16[640,512]{1,0:T(8,128)(2,1)}, u32[]{:S(2)}) copy-start(bf16[640,512]{1,0:T(8,128)(2,1)} %refs_2_.1) | copy-start | bytes 1966084
  28.3 22.1 %copy-start.1 = (bf16[640,512]{1,0:T(8,128)(2,1)S(1)}, bf16[640,512]{1,0:T(8,128)(2,1)}, u32[]{:S(2)}) copy-start(bf16[640,512]{1,0:T(8,128)(2,1)} %refs_3_.1) | copy-start | bytes 1966084
  28.3 21.3 %collective-permute-start.1 = (bf16[640,512]{1,0:T(8,128)(2,1)S(1)}, bf16[640,512]{1,0:T(8,128)(2,1)S(1)}, u32[]{:S(2)}, u32[]{:S(2)}) collective-permute-start(bf16[640,512]{1,0:T(8,128)(2,1)S(1)} %collective-permute-done.refs_8_), channel_id=1, source_target_pairs={{0,4},{4,0},{1,5},{5,1},{2,6},{6,2},{3,7},{7,3}} | collective-permute-start | bytes 1966088 | tf_op jit(solution)/shard_map/ppermute | solution.py:386
  28.6 21.3 %collective-permute-start.2 = (bf16[512,640]{1,0:T(8,128)(2,1)S(1)}, bf16[512,640]{1,0:T(8,128)(2,1)S(1)}, u32[]{:S(2)}, u32[]{:S(2)}) collective-permute-start(bf16[512,640]{1,0:T(8,128)(2,1)S(1)} %copy-done.5), channel_id=1, source_target_pairs={{0,2},{1,3},{2,0},{3,1},{4,6},{5,7},{6,4},{7,5}} | collective-permute-start | bytes 1966088 | tf_op jit(solution)/shard_map/ppermute | solution.py:387
  49.7 2.9 %collective-permute-start.6 = (bf16[640,512]{1,0:T(8,128)(2,1)S(1)}, bf16[640,512]{1,0:T(8,128)(2,1)S(1)}, u32[]{:S(2)}, u32[]{:S(2)}) collective-permute-start(bf16[640,512]{1,0:T(8,128)(2,1)S(1)} %collective-permute-done.refs_8_), channel_id=1, source_target_pairs={{0,1},{1,0},{2,3},{3,2},{4,5},{5,4},{6,7},{7,6}} | collective-permute-start | bytes 1966088 | tf_op jit(solution)/shard_map/ppermute | solution.py:388
  49.9 2.8 %collective-permute-start.7 = (bf16[640,512]{1,0:T(8,128)(2,1)S(1)}, bf16[640,512]{1,0:T(8,128)(2,1)S(1)}, u32[]{:S(2)}, u32[]{:S(2)}) collective-permute-start(bf16[640,512]{1,0:T(8,128)(2,1)S(1)} %collective-permute-done.1.refs_9_), channel_id=1, source_target_pairs={{0,1},{1,0},{2,3},{3,2},{4,5},{5,4},{6,7},{7,6}} | collective-permute-start | bytes 1966088 | tf_op jit(solution)/shard_map/ppermute | solution.py:391
  50.2 3.5 %collective-permute-start.8 = (bf16[512,640]{1,0:T(8,128)(2,1)S(1)}, bf16[512,640]{1,0:T(8,128)(2,1)S(1)}, u32[]{:S(2)}, u32[]{:S(2)}) collective-permute-start(bf16[512,640]{1,0:T(8,128)(2,1)S(1)} %collective-permute-done.2.refs_10_), channel_id=1, source_target_pairs={{0,1},{1,0},{2,3},{3,2},{4,5},{5,4},{6,7},{7,6}} | collective-permute-start | bytes 1966088 | tf_op jit(solution)/shard_map/ppermute | solution.py:392

commit v3 on v2

--- a/solution.py
+++ b/solution.py
@@ -14,10 +14,12 @@
 GROUP = 16
 RING = 4
 TABLE = 512
-
-
-def VIA_XLU(b):
-    return b % 2 == 0
+LEAD = 4 * GROUP
+
+
+def turned(b):
+    return b % 4 != 0
+
 
 BLOCK = 128
 STACK = HEADS * GROUP
@@ -42,6 +44,40 @@
     return jnp.concatenate([t] * HEADS, axis=0)
 
 
+def build_table(rows, cache_size, perm_row, slen_row, table):
+    lane = lax.broadcasted_iota(jnp.int32, (1, TABLE), 1)
+
+    def shifted(row):
+        wide = jnp.concatenate([row, jnp.zeros((1, TABLE - rows), jnp.int32)], axis=1)
+        return pltpu.roll(wide, LEAD, 1)
+
+    def ahead(row, n):
+        return pltpu.roll(row, TABLE - n, 1)
+
+    real = jnp.logical_and(lane >= LEAD, lane < LEAD + rows)
+    blocks = shifted(jnp.maximum((slen_row + (BLOCK - 1)) >> 7, 1))
+    for step in (8, 4, 2, 1):
+        blocks = jnp.where((lane & (GROUP - 1)) + step < GROUP, jnp.maximum(blocks, ahead(blocks, step)), blocks)
+    k_blocks = ahead(blocks, LEAD)
+    v_blocks = jnp.maximum(blocks, 1)
+    v_blocks = jnp.where(k_blocks - v_blocks > 1, k_blocks, v_blocks)
+    padded = (shifted(slen_row) + 15) & -16
+    k_size = jnp.where(real, jnp.maximum(jnp.maximum(padded, 16), (blocks - 1) * BLOCK), 0)
+    v_size = jnp.where(real, jnp.maximum(jnp.maximum(padded, 16), (v_blocks - 1) * BLOCK), 0)
+    k_total, v_total = k_size, v_size
+    for step in (1, 2, 4, 8):
+        k_total = k_total + ahead(k_total, step)
+        v_total = v_total + ahead(v_total, step)
+    table[...] = jnp.zeros(table.shape, jnp.int32)
+    table[0:1, :] = shifted(perm_row * cache_size)
+    table[1:2, :] = k_size
+    table[2:3, :] = v_size
+    table[3:4, :] = v_blocks * 8 + k_blocks
+    table[5:6, :] = k_total
+    table[6:7, :] = v_total
+    table[4:5, :rows] = perm_row
+
+
 def attend_groups(parity, count, cache_size, table, k_hbm, v_hbm, kbuf, vbuf, ksem, vsem, s_buf, p_buf, pn_buf,
                   load_q, load_k, load_v, load_len, store, prepare):
     max_nb = cache_size // BLOCK
@@ -52,64 +88,51 @@
     def slot_row(p, b):
         return pl.multiple_of(((p & (RING - 1)) * GROUP + b) * cache_size, cache_size)
 
-    def issue(hbm, buf, sems, p):
+    def issue(which, p):
+        hbm, buf, sems = ((k_hbm, kbuf, ksem), (v_hbm, vbuf, vsem))[which]
         for b in range(GROUP):
-            src = pl.multiple_of(table[0, first_row(p) + b], cache_size)
-            size = pl.multiple_of(table[1, first_row(p) + b], 16)
+            src = pl.multiple_of(table[0, first_row(p) + (LEAD + b)], cache_size)
+            size = pl.multiple_of(table[1 + which, first_row(p) + (LEAD + b)], 16)
             pltpu.make_async_copy(hbm.at[pl.ds(src, size)], buf.at[pl.ds(slot_row(p, b), size)],
                                   sems.at[p & (RING - 1)]).start()
 
-    def wait(hbm, buf, sems, p):
-        n = pl.multiple_of(table[3, first_row(p)], 16)
+    def wait(which, p):
+        hbm, buf, sems = ((k_hbm, kbuf, ksem), (v_hbm, vbuf, vsem))[which]
+        n = pl.multiple_of(table[5 + which, first_row(p) + LEAD], 16)
         pltpu.make_async_copy(hbm.at[pl.ds(0, n)], buf.at[pl.ds(0, n)], sems.at[p & (RING - 1)]).wait()
 
-    def blocks(p):
-        return (table[1, first_row(p)] + (BLOCK - 1)) >> 7
-
-    zeros = jnp.zeros((BLOCK, HEAD_DIM), BF16)
-
-    def fill(p, c):
-        upto = jnp.where(p < 1, max_nb, blocks(jnp.maximum(p - 1, 0)))
-        for b in range(GROUP):
-            base = slot_row(p, b)
-            own = (table[1, first_row(p) + b] + (BLOCK - 1)) >> 7
-
-            def clear(t, c):
-                at = pl.multiple_of(base + t * BLOCK, BLOCK)
-                kbuf[pl.ds(at, BLOCK), :] = zeros
-                vbuf[pl.ds(at, BLOCK), :] = zeros
-                return c
-            lax.fori_loop(own - 1, upto, clear, 0)
-        issue(k_hbm, kbuf, ksem, p)
-        issue(v_hbm, vbuf, vsem, p)
-        return c
-    lax.fori_loop(0, RING, fill, 0)
+    token = lax.broadcasted_iota(jnp.int32, (BLOCK, HEAD_DIM), 0).astype(BF16)
+
+    def read(which, p, b, nb):
+        buf = (kbuf, vbuf)[which]
+        at = slot_row(p, b)
+        left = table[1 + which, first_row(p) + (LEAD + b)] - (nb - 1) * BLOCK
+        tail = buf[pl.ds(at + (nb - 1) * BLOCK, BLOCK), :]
+        tail = jnp.where(token < left.astype(F32).astype(BF16), tail, jnp.zeros_like(tail))
+        if nb == 1:
+            return tail
+        return jnp.concatenate([buf[pl.ds(at, (nb - 1) * BLOCK), :], tail], axis=0)
+
+    for p in range(3):
+        issue(0, p)
+    issue(1, 0)
 
     prepare()
 
-    def scores(p, nb):
-        q = load_q(2 * p + parity)
-        member = lax.broadcasted_iota(jnp.int32, (STACK, HEAD_DIM), 0) % GROUP
-        out = None
-        for b in range(GROUP):
-            k_b = kbuf[pl.ds(slot_row(p, b), nb * BLOCK), :]
-            q_b = jnp.where(member == b, q, jnp.zeros_like(q))
-            if VIA_XLU(b):
-                k_t = k_b.T
-                lane = lax.broadcasted_iota(jnp.int32, k_t.shape, 1)
-                part = dot(q_b, jnp.where(lane < table[1, first_row(p) + b], k_t, jnp.zeros_like(k_t)))
-            else:
-                part = dot_t(q_b, k_b)
-            out = part if out is None else out + part
-        return out
-
-    def softmax(p, s):
-        width = s.shape[1]
+    def score_part(p, b, nb, q, member):
+        q_b = jnp.where(member == b, q, jnp.zeros_like(q))
+        if turned(b):
+            k_t = kbuf[pl.ds(slot_row(p, b), nb * BLOCK), :].T
+            lane = lax.broadcasted_iota(jnp.int32, k_t.shape, 1)
+            return dot(q_b, jnp.where(lane < table[1, first_row(p) + (LEAD + b)], k_t, jnp.zeros_like(k_t)))
+        return dot_t(q_b, read(0, p, b, nb))
+
+    def softmax(p):
         start = pl.multiple_of(first_row(p), GROUP)
         lens = tile_heads(load_len(start))[:, :1]
-        valid = lax.broadcasted_iota(jnp.int32, (STACK, width), 1).astype(F32) < lens
+        valid = lax.broadcasted_iota(jnp.int32, s_buf.shape, 1).astype(F32) < lens
         s_new = jnp.sum(load_q(2 * p + parity).astype(F32) * tile_heads(load_k(start)), axis=-1, keepdims=True)
-        s = jnp.where(valid, s, -jnp.inf)
+        s = jnp.where(valid, s_buf[...], -jnp.inf)
         peak = jnp.maximum(jnp.max(s, axis=-1, keepdims=True), s_new)
         w = jnp.exp(s - peak)
         w_new = jnp.exp(s_new - peak)
@@ -117,42 +140,41 @@
         prob_new = (w_new * inv).astype(BF16).astype(F32)
         return (w * inv).astype(BF16), jnp.broadcast_to(prob_new, (STACK, 128))
 
-    def values(p, prob, prob_new):
-        width = prob.shape[1]
-        start = pl.multiple_of(first_row(p), GROUP)
-        member = lax.broadcasted_iota(jnp.int32, (STACK, width), 0) % GROUP
-        out = None
+    def work(p, v_nb, k_nb):
+        prob, prob_new = softmax(jnp.maximum(p + 1, 0))
+        q = load_q(2 * (p + 2) + parity)
+        member_q = lax.broadcasted_iota(jnp.int32, (STACK, HEAD_DIM), 0) % GROUP
+        old = p_buf[:, :v_nb * BLOCK]
+        member = lax.broadcasted_iota(jnp.int32, old.shape, 0) % GROUP
+        s, out = None, None
         for b in range(GROUP):
-            part = dot(jnp.where(member == b, prob, jnp.zeros_like(prob)), vbuf[pl.ds(slot_row(p, b), width), :])
+            if k_nb:
+                part = score_part(p + 2, b, k_nb, q, member_q)
+                s = part if s is None else s + part
+            part = dot(jnp.where(member == b, old, jnp.zeros_like(old)), read(1, p, b, v_nb))
             out = part if out is None else out + part
-        store(p, out + prob_new[:, :1] * tile_heads(load_v(start)))
-
-    wait(k_hbm, kbuf, ksem, 0)
-    s_buf[...] = scores(0, max_nb)
-    issue(k_hbm, kbuf, ksem, RING)
-
-    def step(p, c):
-        nb_p = blocks(p)
-        wait(k_hbm, kbuf, ksem, p + 1)
-        for nb in range(1, max_nb + 1):
-            @pl.when(nb_p == nb)
+        start = pl.multiple_of(first_row(jnp.maximum(p, 0)), GROUP)
+        store(p + 2, out + pn_buf[:, :1] * tile_heads(load_v(start)))
+        if k_nb:
+            s_buf[:, :k_nb * BLOCK] = s
+        p_buf[...] = prob
+        pn_buf[...] = prob_new
+
+    variants = [(v, k) for v in range(1, max_nb + 1) for k in (0, v, v + 1) if k <= max_nb]
+
+    def step(i, c):
+        p = i - 2
+        wait(0, p + 2)
+        wait(1, p)
+        issue(1, p + 3)
+        issue(0, p + 5)
+        code = table[3, first_row(p) + LEAD]
+        for v, k in variants:
+            @pl.when(code == v * 8 + k)
             def _():
-                width = nb * BLOCK
-                nxt = scores(p + 1, nb)
-                prob, prob_new = softmax(p, s_buf[:, :width])
-                s_buf[:, :width] = nxt
-                p_buf[:, :width] = prob
-                pn_buf[...] = prob_new
-        issue(k_hbm, kbuf, ksem, p + 1 + RING)
-        wait(v_hbm, vbuf, vsem, p)
-        for nb in range(1, max_nb + 1):
-            @pl.when(nb_p == nb)
-            def _():
-                width = nb * BLOCK
-                values(p, p_buf[:, :width], pn_buf[...])
-        issue(v_hbm, vbuf, vsem, p + RING)
+                work(p, v, k)
         return c
-    lax.fori_loop(0, count, step, 0)
+    lax.fori_loop(0, count + 2, step, 0)
 
 
 def first_kernel(rows, cache_size, x_in, len_in, na_ref, wq, wk, wv, k_hbm, v_hbm,
@@ -162,25 +184,17 @@
 
     len_row = len_in[...].astype(F32)
     lane_id = lax.broadcasted_iota(jnp.int32, (1, rows), 1).astype(F32)
-    key_row = len_row * rows + (rows - 1 - lane_id)
+    key_row = len_row * rows + lane_id
     key_col = jnp.broadcast_to(key_row, (128, rows)).T[:, :1]
     len_col = jnp.broadcast_to(len_row, (128, rows)).T[:, :1]
     sub_id = lax.broadcasted_iota(jnp.int32, (rows, rows), 0).astype(F32)
     lane_sq = lax.broadcasted_iota(jnp.int32, (rows, rows), 1).astype(F32)
-    rank_row = jnp.sum((key_col > key_row).astype(F32), axis=0, keepdims=True)
-    rank_col = jnp.sum((key_row > key_col).astype(F32), axis=1, keepdims=True)
+    rank_row = jnp.sum((key_col < key_row).astype(F32), axis=0, keepdims=True)
+    rank_col = jnp.sum((key_row < key_col).astype(F32), axis=1, keepdims=True)
     to_natural = rank_col == lane_sq
     perm_row = jnp.sum(jnp.where(to_natural, sub_id, 0.0), axis=0, keepdims=True).astype(jnp.int32)
     slen_row = jnp.sum(jnp.where(to_natural, len_col, 0.0), axis=0, keepdims=True).astype(jnp.int32)
-    table_out[...] = jnp.zeros(table_out.shape, jnp.int32)
-    size_row = jnp.maximum((slen_row + 15) & -16, 16)
-    group_row = size_row
-    for shift in (1, 2, 4, 8):
-        group_row = group_row + pltpu.roll(group_row, rows - shift, 1)
-    table_out[0:1, :rows] = perm_row * cache_size
-    table_out[1:2, :rows] = size_row
-    table_out[2:3, :rows] = perm_row
-    table_out[3:4, :rows] = group_row
+    build_table(rows, cache_size, perm_row, slen_row, table_out)
     table_copy = pltpu.make_async_copy(table_out, table, tsem)
     table_copy.start()
     table_copy.wait()
@@ -240,11 +254,11 @@
                   lambda g: q_in[g].astype(BF16), lambda s: ks_in[pl.ds(s, GROUP), :], lambda s: vs_in[pl.ds(s, GROUP), :],
                   lambda s: len_in[pl.ds(s, GROUP), :], store, prepare)
 
-    perm = tab_in[2:3, :rows]
+    perm = tab_in[4:5, :rows]
     natural = lax.broadcasted_iota(jnp.int32, (rows, rows), 0)
     back = (natural == perm).astype(BF16)
-    o_all = jnp.concatenate([o_even[...].reshape(groups // 2, GROUP, HEADS * HEAD_DIM),
-                             o_odd[...].reshape(groups // 2, GROUP, HEADS * HEAD_DIM)], axis=1).reshape(rows, HEADS * HEAD_DIM).astype(BF16)
+    o_all = jnp.concatenate([o_even[2 * GROUP:, :].reshape(groups // 2, GROUP, HEADS * HEAD_DIM),
+                             o_odd[2 * GROUP:, :].reshape(groups // 2, GROUP, HEADS * HEAD_DIM)], axis=1).reshape(rows, HEADS * HEAD_DIM).astype(BF16)
     mixed = dot(dot(back, o_all).astype(BF16), wo[...])
     x1 = x_in[...].astype(F32) + mixed
     x1_ref[...] = x1
@@ -278,7 +292,7 @@
         functools.partial(first_kernel, rows, cache_size),
         out_shape=(shape((rows, HEAD_DIM), BF16), shape((rows, HEAD_DIM), BF16), shape((8, TABLE), jnp.int32),
                    shape((groups + 4, STACK, HEAD_DIM), F32), shape((rows + 2 * GROUP, HEAD_DIM), F32), shape((rows + 2 * GROUP, HEAD_DIM), F32),
-                   shape((rows + 2 * GROUP, 128), F32), shape((rows // 2, width), F32)),
+                   shape((rows + 2 * GROUP, 128), F32), shape((rows // 2 + 2 * GROUP, width), F32)),
         in_specs=[VMEM_SPEC] * 6 + [HBM_SPEC] * 2,
         out_specs=(VMEM_SPEC,) * 8,
         scratch_shapes=ring_scratch(cache_size) + [
@@ -309,7 +323,7 @@
         in_specs=[SMEM_SPEC] + [VMEM_SPEC] * 9 + [HBM_SPEC] * 2,
         out_specs=(VMEM_SPEC,) * 2,
         scratch_shapes=ring_scratch(cache_size) + [
-            pltpu.VMEM((rows // 2, width), F32),
+            pltpu.VMEM((rows // 2 + 2 * GROUP, width), F32),
             pltpu.VMEM((STACK, cache_size), F32),
             pltpu.VMEM((STACK, cache_size), BF16),
             pltpu.VMEM((STACK, 128), F32),

time: 55.4 us -> 48.1 us (0.87)
  Pallas kernels: 44.8 us -> 37.2 us
    pallas_call x1, Pallas kernels: 19.7 us -> 15.9 us  [attention_second(): pl.pallas_call(functools.partial(second_kernel, rows, cache_size), out_sh...]
    pallas_call x1, Pallas kernels: 21.5 us -> 17.7 us  [attention_first(): pl.pallas_call(functools.partial(first_kernel, rows, cache_size), out_sha...]
    ppermute x1, starting transfers between devices: 0.26 us -> 1.56 us  [per_device(): other_far = lax.ppermute(half_far, 'dp', ROWS)]
    ppermute x1, starting transfers between devices: 1.39 us -> 0.5 us  [per_device(): down_far = lax.ppermute(down_own, 'tp', ACROSS)]
  transfers between devices with their start and end apart: 9 -> 9, of which waited for: 2 -> 2; matrix products, arithmetic and copies ran while one was open for 2% -> 2% of each run, Pallas kernels for 78% -> 74%
where the time goes in v3:
time: 48.1 us
  Pallas kernels  37.2 us (77%)
  starting transfers between devices  6.54 us (14%)
  waiting for transfers between devices  1.29 us (3%)
  other arithmetic  1.16 us (2%)
  local copies, waits for them, and re-layouts  1.02 us (2%)
  between operations  0.84 us (2%)
    pallas_call x1, Pallas kernels, attention_first(): pl.pallas_call(functools.partial(first_kernel, rows, cache_size), out_sha...  17.7 us
    pallas_call x1, Pallas kernels, attention_second(): pl.pallas_call(functools.partial(second_kernel, rows, cache_size), out_sh...  15.9 us
    pallas_call x2, Pallas kernels, mlp(): pl.pallas_call(functools.partial(mlp_kernel, n, last, swap_at), out_shape...  3.67 us
    ppermute x1, starting transfers between devices, per_device(): half_far = lax.ppermute(half, 'tp', ACROSS)  3.02 us
    ppermute x1, starting transfers between devices, per_device(): other_far = lax.ppermute(half_far, 'dp', ROWS)  1.56 us
    select_n x1, other arithmetic, per_device(): half = jnp.where(lax.axis_index('dp') == 0, w_gate, w_up)  1.16 us
    unnamed x22, local copies, waits for them, and re-layouts  1.01 us
  transfers between devices with their start and end apart: 9, of which 2 were waited for; matrix products, arithmetic and copies ran while one was open for 2% of the time, Pallas kernels for 74%

profile of v3, /device:TPU:0, one launch (start us, length us, event | category | flops | bytes accessed | tf_op | source)
XLA Modules:
  0.0 48.1 jit_solution(11029957207492022414)
XLA Ops:
  0.6 0.0 copy-start.9
  0.6 0.0 copy-start.10
  0.7 0.0 copy-start.8
  0.7 0.0 copy-start.4
  0.7 0.9 %collective-permute-start.3 = (bf16[640,512]{1,0:T(8,128)(2,1)}, bf16[640,512]{1,0:T(8,128)(2,1)S(1)}, u32[]{:S(2)}, u32[]{:S(2)}) collective-permute-start(bf16[640,512]{1,0:T(8,128)(2,1)} %refs_2_.1), channel_id=1, source_target_pairs={{0,1},{1,0},{2,3},{3,2},{4,5},{5,4},{6,7},{7,6}} | collective-permute-start | bytes 1966088 | tf_op jit(solution)/shard_map/ppermute | solution.py:397
  1.6 0.0 collective-permute-start.4
  1.6 1.2 %broadcast_select_fusion = bf16[640,512]{1,0:T(8,128)(2,1)S(1)} fusion(bf16[640,512]{1,0:T(8,128)(2,1)} %refs_2_.1, bf16[640,512]{1,0:T(8,128)(2,1)} %refs_3_.1, pred[]{:T(512)S(6)} %eq.3), kind=kLoop, calls=%fused_computation | loop fusion | flops 327680 | bytes 1966081 | tf_op jit(solution)/shard_map/jit(_where)/select_n | solution.py:395
  2.8 3.0 %collective-permute-start = (bf16[640,512]{1,0:T(8,128)(2,1)S(1)}, bf16[640,512]{1,0:T(8,128)(2,1)S(1)}, u32[]{:S(2)}, u32[]{:S(2)}) collective-permute-start(bf16[640,512]{1,0:T(8,128)(2,1)S(1)} %broadcast_select_fusion), channel_id=1, source_target_pairs={{0,2},{1,3},{2,0},{3,1},{4,6},{5,7},{6,4},{7,5}} | collective-permute-start | bytes 1966088 | tf_op jit(solution)/shard_map/ppermute | solution.py:396
  5.8 0.0 collective-permute-start.5
  5.9 0.0 copy-start.7
  5.9 1.0 %copy-done.7 = bf16[640,256]{1,0:T(8,128)(2,1)S(1)} copy-done((bf16[640,256]{1,0:T(8,128)(2,1)S(1)}, bf16[640,256]{1,0:T(8,128)(2,1)}, u32[]{:S(2)}) %copy-start.7) | copy-done | bytes 327704
  6.8 17.7 %attention_first.1 = (bf16[256,256]{1,0:T(8,128)(2,1)}, bf16[256,256]{1,0:T(8,128)(2,1)}, s32[8,512]{1,0:T(8,128)S(1)}, f32[20,64,256]{2,1,0:T(8,128)S(1)}, f32[...) custom-call(bf16[256,640]{1,0:T(8,128)(2,1)S(1)} %copy-done.4, ...), custom_call_target="tpu_custom_call" | custom-call | flops 10000000000 | bytes 40000000 | tf_op jit(solution)/shard_map/attention_first/pallas_call | solution.py:291
  24.5 0.0 collective-permute-done.refs_8_
  24.6 0.0 copy-start
  24.6 0.0 copy-start.1
  24.6 1.6 %collective-permute-start.1 = (bf16[640,512]{1,0:T(8,128)(2,1)S(1)}, bf16[640,512]{1,0:T(8,128)(2,1)S(1)}, u32[]{:S(2)}, u32[]{:S(2)}) collective-permute-start(bf16[640,512]{1,0:T(8,128)(2,1)S(1)} %collective-permute-done.refs_8_), channel_id=1, source_target_pairs={{0,4},{4,0},{1,5},{5,1},{2,6},{6,2},{3,7},{7,3}} | collective-permute-start | bytes 1966088 | tf_op jit(solution)/shard_map/ppermute | solution.py:400
  26.1 0.5 %collective-permute-start.2 = (bf16[512,640]{1,0:T(8,128)(2,1)S(1)}, bf16[512,640]{1,0:T(8,128)(2,1)S(1)}, u32[]{:S(2)}, u32[]{:S(2)}) collective-permute-start(bf16[512,640]{1,0:T(8,128)(2,1)S(1)} %copy-done.5), channel_id=1, source_target_pairs={{0,2},{1,3},{2,0},{3,1},{4,6},{5,7},{6,4},{7,5}} | collective-permute-start | bytes 1966088 | tf_op jit(solution)/shard_map/ppermute | solution.py:401
  26.6 15.9 %attention_second.1 = (f32[256,640]{1,0:T(8,128)S(1)}, bf16[256,640]{1,0:T(8,128)(2,1)S(1)}) custom-call(s32[8,512]{1,0:T(8,128)S(1)} %get-tuple-element.33.table.tab_in, bf16[256,640]{1,0:T(8,128)(2,1)S(1)} %copy-done.4, f32[20,64,256]{2,1,0:T(8,128)S(1)} %get-tuple-element.34.q_in, f32[288,256]{1,0:T(8,128)S(1)} %get-tuple-element.35.ks_in, ...), custom_call_target="tpu_custom_call" | custom-call | flops 10000000000 | bytes 40000000 | tf_op jit(solution)/shard_map/attention_second/pallas_call | solution.py:320
  42.5 0.0 collective-permute-done.1.refs_9_
  42.5 0.0 collective-permute-start.6
  42.6 0.4 collective-permute-done.2.refs_10_
  42.9 0.1 collective-permute-start.7
  43.1 0.0 collective-permute-done.3.refs_5_
  43.1 0.4 collective-permute-start.8
  43.5 0.0 collective-permute-done.4.refs_6_
  43.5 0.0 collective-permute-done.5.refs_7_
  43.5 0.0 copy-done.1
  43.5 2.1 %mlp.2.refs_0_ = f32[256,640]{1,0:T(8,128)S(1)} custom-call(f32[256,640]{1,0:T(8,128)S(1)} %get-tuple-element.41.refs_0_, bf16[256,640]{1,0:T(8,128)(2,1)S(1)} %get-tuple-element.42.refs_1_, bf16[640,512]{1,0:T(8,128)(2,1)S(1)} %copy-done, bf16[640,512]{1,0:T(8,128)(2,1)S(1)} %copy-done.1, bf16[512,640]{1,0:T(8,128)(2,1)S(1)} %copy-done.5, ...), custom_call_target="tpu_custom_call" | custom-call | flops 1509949440 | bytes 5898240 | tf_op jit(solution)/shard_map/mlp/pallas_call | solution.py:372
  45.6 0.0 collective-permute-done.6.refs_2_
  45.6 0.0 collective-permute-done.7.refs_3_
  45.6 0.9 %collective-permute-done.8.refs_4_ = bf16[512,640]{1,0:T(8,128)(2,1)S(1)} collective-permute-done((bf16[512,640]{1,0:T(8,128)(2,1)S(1)}, bf16[512,640]{1,0:T(8,128)(2,1)S(1)}, u32[]{:S(2)}, u32[]{:S(2)}) %collective-permute-start.8) | collective-permute-done | bytes 655392 | tf_op jit(solution)/shard_map/ppermute | solution.py:406
  46.5 1.6 %mlp.3 = bf16[256,640]{1,0:T(8,128)(2,1)} custom-call(f32[256,640]{1,0:T(8,128)S(1)} %mlp.2.refs_0_, bf16[256,640]{1,0:T(8,128)(2,1)S(1)} %get-tuple-element.42.refs_1_, bf16[640,512]{1,0:T(8,128)(2,1)S(1)} %collective-permute-done.6.refs_2_, bf16[640,512]{1,0:T(8,128)(2,1)S(1)} %collective-permute-done.7.refs_3_, ...), custom_call_target="tpu_custom_call" | custom-call | flops 503316480 | bytes 1966080 | tf_op jit(solution)/shard_map/mlp/pallas_call | solution.py:372
  (15 shorter events, 0.0 us)
Async XLA Ops:
  0.6 5.2 %copy-start.9 = (bf16[640]{0:T(1024)(128)(2,1)S(1)}, bf16[640]{0:T(1024)(128)(2,1)}, u32[]{:S(2)}) copy-start(bf16[640]{0:T(1024)(128)(2,1)} %param.17) | copy-start | bytes 3844
  0.6 5.2 %copy-start.10 = (bf16[640]{0:T(1024)(128)(2,1)S(1)}, bf16[640]{0:T(1024)(128)(2,1)}, u32[]{:S(2)}) copy-start(bf16[640]{0:T(1024)(128)(2,1)} %param.18) | copy-start | bytes 3844
  0.7 5.2 %copy-start.8 = (s32[256]{0:T(256)S(1)}, s32[256]{0:T(256)}, u32[]{:S(2)}) copy-start(s32[256]{0:T(256)} %param.16) | copy-start | bytes 3076
  0.7 5.2 %copy-start.4 = (bf16[256,640]{1,0:T(8,128)(2,1)S(1)}, bf16[256,640]{1,0:T(8,128)(2,1)}, u32[]{:S(2)}) copy-start(bf16[256,640]{1,0:T(8,128)(2,1)} %x_in.3) | copy-start | bytes 983044
  0.7 5.2 %copy-start.2 = (bf16[640,1024]{1,0:T(8,128)(2,1)S(1)}, bf16[640,1024]{1,0:T(8,128)(2,1)}, u32[]{:S(2)}) copy-start(bf16[640,1024]{1,0:T(8,128)(2,1)} %wq.1) | copy-start | bytes 3932164
  0.7 5.2 %copy-start.6 = (bf16[640,256]{1,0:T(8,128)(2,1)S(1)}, bf16[640,256]{1,0:T(8,128)(2,1)}, u32[]{:S(2)}) copy-start(bf16[640,256]{1,0:T(8,128)(2,1)} %wk.1) | copy-start | bytes 983044
  0.7 42.4 %collective-permute-start.3 = (bf16[640,512]{1,0:T(8,128)(2,1)}, bf16[640,512]{1,0:T(8,128)(2,1)S(1)}, u32[]{:S(2)}, u32[]{:S(2)}) collective-permute-start(bf16[640,512]{1,0:T(8,128)(2,1)} %refs_2_.1), channel_id=1, source_target_pairs={{0,1},{1,0},{2,3},{3,2},{4,5},{5,4},{6,7},{7,6}} | collective-permute-start | bytes 1966088 | tf_op jit(solution)/shard_map/ppermute | solution.py:397
  1.6 41.9 %collective-permute-start.4 = (bf16[640,512]{1,0:T(8,128)(2,1)}, bf16[640,512]{1,0:T(8,128)(2,1)S(1)}, u32[]{:S(2)}, u32[]{:S(2)}) collective-permute-start(bf16[640,512]{1,0:T(8,128)(2,1)} %refs_3_.1), channel_id=1, source_target_pairs={{0,1},{1,0},{2,3},{3,2},{4,5},{5,4},{6,7},{7,6}} | collective-permute-start | bytes 1966088 | tf_op jit(solution)/shard_map/ppermute | solution.py:397
  2.8 21.8 %collective-permute-start = (bf16[640,512]{1,0:T(8,128)(2,1)S(1)}, bf16[640,512]{1,0:T(8,128)(2,1)S(1)}, u32[]{:S(2)}, u32[]{:S(2)}) collective-permute-start(bf16[640,512]{1,0:T(8,128)(2,1)S(1)} %broadcast_select_fusion), channel_id=1, source_target_pairs={{0,2},{1,3},{2,0},{3,1},{4,6},{5,7},{6,4},{7,5}} | collective-permute-start | bytes 1966088 | tf_op jit(solution)/shard_map/ppermute | solution.py:396
  5.8 37.7 %collective-permute-start.5 = (bf16[512,640]{1,0:T(8,128)(2,1)}, bf16[512,640]{1,0:T(8,128)(2,1)S(1)}, u32[]{:S(2)}, u32[]{:S(2)}) collective-permute-start(bf16[512,640]{1,0:T(8,128)(2,1)} %refs_4_.1), channel_id=1, source_target_pairs={{0,1},{1,0},{2,3},{3,2},{4,5},{5,4},{6,7},{7,6}} | collective-permute-start | bytes 1966088 | tf_op jit(solution)/shard_map/ppermute | solution.py:397
  5.9 1.0 %copy-start.7 = (bf16[640,256]{1,0:T(8,128)(2,1)S(1)}, bf16[640,256]{1,0:T(8,128)(2,1)}, u32[]{:S(2)}) copy-start(bf16[640,256]{1,0:T(8,128)(2,1)} %wv.1) | copy-start | bytes 983044
  6.8 19.3 %copy-start.5 = (bf16[512,640]{1,0:T(8,128)(2,1)S(1)}, bf16[512,640]{1,0:T(8,128)(2,1)}, u32[]{:S(2)}) copy-start(bf16[512,640]{1,0:T(8,128)(2,1)} %refs_4_.1) | copy-start | bytes 1966084
  6.8 19.8 %copy-start.3 = (bf16[1024,640]{1,0:T(8,128)(2,1)S(1)}, bf16[1024,640]{1,0:T(8,128)(2,1)}, u32[]{:S(2)}) copy-start(bf16[1024,640]{1,0:T(8,128)(2,1)} %wo.1) | copy-start | bytes 3932164
  24.6 18.9 %copy-start = (bf16[640,512]{1,0:T(8,128)(2,1)S(1)}, bf16[640,512]{1,0:T(8,128)(2,1)}, u32[]{:S(2)}) copy-start(bf16[640,512]{1,0:T(8,128)(2,1)} %refs_2_.1) | copy-start | bytes 1966084
  24.6 18.9 %copy-start.1 = (bf16[640,512]{1,0:T(8,128)(2,1)S(1)}, bf16[640,512]{1,0:T(8,128)(2,1)}, u32[]{:S(2)}) copy-start(bf16[640,512]{1,0:T(8,128)(2,1)} %refs_3_.1) | copy-start | bytes 1966084
  24.6 18.0 %collective-permute-start.1 = (bf16[640,512]{1,0:T(8,128)(2,1)S(1)}, bf16[640,512]{1,0:T(8,128)(2,1)S(1)}, u32[]{:S(2)}, u32[]{:S(2)}) collective-permute-start(bf16[640,512]{1,0:T(8,128)(2,1)S(1)} %collective-permute-done.refs_8_), channel_id=1, source_target_pairs={{0,4},{4,0},{1,5},{5,1},{2,6},{6,2},{3,7},{7,3}} | collective-permute-start | bytes 1966088 | tf_op jit(solution)/shard_map/ppermute | solution.py:400
  26.1 16.8 %collective-permute-start.2 = (bf16[512,640]{1,0:T(8,128)(2,1)S(1)}, bf16[512,640]{1,0:T(8,128)(2,1)S(1)}, u32[]{:S(2)}, u32[]{:S(2)}) collective-permute-start(bf16[512,640]{1,0:T(8,128)(2,1)S(1)} %copy-done.5), channel_id=1, source_target_pairs={{0,2},{1,3},{2,0},{3,1},{4,6},{5,7},{6,4},{7,5}} | collective-permute-start | bytes 1966088 | tf_op jit(solution)/shard_map/ppermute | solution.py:401
  42.5 3.1 %collective-permute-start.6 = (bf16[640,512]{1,0:T(8,128)(2,1)S(1)}, bf16[640,512]{1,0:T(8,128)(2,1)S(1)}, u32[]{:S(2)}, u32[]{:S(2)}) collective-permute-start(bf16[640,512]{1,0:T(8,128)(2,1)S(1)} %collective-permute-done.refs_8_), channel_id=1, source_target_pairs={{0,1},{1,0},{2,3},{3,2},{4,5},{5,4},{6,7},{7,6}} | collective-permute-start | bytes 1966088 | tf_op jit(solution)/shard_map/ppermute | solution.py:402
  42.9 2.7 %collective-permute-start.7 = (bf16[640,512]{1,0:T(8,128)(2,1)S(1)}, bf16[640,512]{1,0:T(8,128)(2,1)S(1)}, u32[]{:S(2)}, u32[]{:S(2)}) collective-permute-start(bf16[640,512]{1,0:T(8,128)(2,1)S(1)} %collective-permute-done.1.refs_9_), channel_id=1, source_target_pairs={{0,1},{1,0},{2,3},{3,2},{4,5},{5,4},{6,7},{7,6}} | collective-permute-start | bytes 1966088 | tf_op jit(solution)/shard_map/ppermute | solution.py:405
  43.1 3.5 %collective-permute-start.8 = (bf16[512,640]{1,0:T(8,128)(2,1)S(1)}, bf16[512,640]{1,0:T(8,128)(2,1)S(1)}, u32[]{:S(2)}, u32[]{:S(2)}) collective-permute-start(bf16[512,640]{1,0:T(8,128)(2,1)S(1)} %collective-permute-done.2.refs_10_), channel_id=1, source_target_pairs={{0,1},{1,0},{2,3},{3,2},{4,5},{5,4},{6,7},{7,6}} | collective-permute-start | bytes 1966088 | tf_op jit(solution)/shard_map/ppermute | solution.py:406

commit v4 on v3

--- a/solution.py
+++ b/solution.py
@@ -394,13 +394,14 @@
     def per_device(hidden_in, k_cache, v_cache, cache_len, norm_attn, norm_mlp, w_q, w_k, w_v, w_o, w_gate, w_up, w_down):
         half = jnp.where(lax.axis_index('dp') == 0, w_gate, w_up)
         half_far = lax.ppermute(half, 'tp', ACROSS)
+        half, down_own = lax.optimization_barrier((half, w_down))
+        down_far = lax.ppermute(down_own, 'tp', ACROSS)
         near = tuple(lax.ppermute(w, 'tp', CORE) for w in (w_gate, w_up, w_down))
         k_new, v_new, *state = attention_first(hidden_in, k_cache, v_cache, cache_len, norm_attn, w_q, w_k, w_v)
-        half_far, down_own, state = lax.optimization_barrier((half_far, w_down, state))
+        half_far, gain_mlp, state = lax.optimization_barrier((half_far, norm_mlp, state))
         other_far = lax.ppermute(half_far, 'dp', ROWS)
-        down_far = lax.ppermute(down_own, 'tp', ACROSS)
         half_diag = lax.ppermute(half_far, 'tp', CORE)
-        x_mid, xn_mid = attention_second(hidden_in, k_cache, v_cache, norm_mlp, w_o, *state)
+        x_mid, xn_mid = attention_second(hidden_in, k_cache, v_cache, gain_mlp, w_o, *state)
         other_far, down_far, x_mid, xn_mid = lax.optimization_barrier((other_far, down_far, x_mid, xn_mid))
         other_diag = lax.ppermute(other_far, 'tp', CORE)
         down_diag = lax.ppermute(down_far, 'tp', CORE)

time: 48.1 us -> 48.1 us (level)
  no operation moved by 1% of the time
where the time goes in v4:
time: 48.1 us; the launch traced here: 47.6 us
  Pallas kernels  36.8 us (77%)
  starting transfers between devices  6.61 us (14%)
  waiting for transfers between devices  1.26 us (3%)
  other arithmetic  1.16 us (2%)
  local copies, waits for them, and re-layouts  1.02 us (2%)
  between operations  0.84 us (2%)
    pallas_call x1, Pallas kernels, attention_first(): pl.pallas_call(functools.partial(first_kernel, rows, cache_size), out_sha...  17.7 us
    pallas_call x1, Pallas kernels, attention_second(): pl.pallas_call(functools.partial(second_kernel, rows, cache_size), out_sh...  15.4 us
    pallas_call x2, Pallas kernels, mlp(): pl.pallas_call(functools.partial(mlp_kernel, n, last, swap_at), out_shape...  3.68 us
    ppermute x1, starting transfers between devices, per_device(): half_far = lax.ppermute(half, 'tp', ACROSS)  3.02 us
    ppermute x1, starting transfers between devices, per_device(): other_far = lax.ppermute(half_far, 'dp', ROWS)  2.04 us
    select_n x1, other arithmetic, per_device(): half = jnp.where(lax.axis_index('dp') == 0, w_gate, w_up)  1.16 us
    unnamed x22, local copies, waits for them, and re-layouts  1.02 us
  transfers between devices with their start and end apart: 9, of which 2 were waited for; matrix products, arithmetic and copies ran while one was open for 2% of the time, Pallas kernels for 74%

profile of v4, /device:TPU:0, one launch (start us, length us, event | category | flops | bytes accessed | tf_op | source)
XLA Modules:
  0.0 47.6 jit_solution(2511103794535678265)
XLA Ops:
  0.6 0.0 copy-start.9
  0.6 0.0 copy-start.8
  0.7 0.0 copy-start.4
  0.7 0.0 copy-start.2
  0.7 0.9 %collective-permute-start.3 = (bf16[640,512]{1,0:T(8,128)(2,1)}, bf16[640,512]{1,0:T(8,128)(2,1)S(1)}, u32[]{:S(2)}, u32[]{:S(2)}) collective-permute-start(bf16[640,512]{1,0:T(8,128)(2,1)} %refs_2_.1), channel_id=1, source_target_pairs={{0,1},{1,0},{2,3},{3,2},{4,5},{5,4},{6,7},{7,6}} | collective-permute-start | bytes 1966088 | tf_op jit(solution)/shard_map/ppermute | solution.py:399
  1.6 0.0 collective-permute-start.4
  1.6 1.2 %broadcast_select_fusion = bf16[640,512]{1,0:T(8,128)(2,1)S(1)} fusion(bf16[640,512]{1,0:T(8,128)(2,1)} %refs_2_.1, bf16[640,512]{1,0:T(8,128)(2,1)} %refs_3_.1, pred[]{:T(512)S(6)} %eq.3), kind=kLoop, calls=%fused_computation | loop fusion | flops 327680 | bytes 1966081 | tf_op jit(solution)/shard_map/jit(_where)/select_n | solution.py:395
  2.8 3.0 %collective-permute-start = (bf16[640,512]{1,0:T(8,128)(2,1)S(1)}, bf16[640,512]{1,0:T(8,128)(2,1)S(1)}, u32[]{:S(2)}, u32[]{:S(2)}) collective-permute-start(bf16[640,512]{1,0:T(8,128)(2,1)S(1)} %broadcast_select_fusion), channel_id=1, source_target_pairs={{0,2},{1,3},{2,0},{3,1},{4,6},{5,7},{6,4},{7,5}} | collective-permute-start | bytes 1966088 | tf_op jit(solution)/shard_map/ppermute | solution.py:396
  5.8 0.0 collective-permute-start.5
  5.8 0.1 collective-permute-start.2
  5.9 0.0 copy-start.7
  5.9 1.0 %copy-done.7 = bf16[640,256]{1,0:T(8,128)(2,1)S(1)} copy-done((bf16[640,256]{1,0:T(8,128)(2,1)S(1)}, bf16[640,256]{1,0:T(8,128)(2,1)}, u32[]{:S(2)}) %copy-start.7) | copy-done | bytes 327704
  6.9 17.7 %attention_first.1 = (bf16[256,256]{1,0:T(8,128)(2,1)}, bf16[256,256]{1,0:T(8,128)(2,1)}, s32[8,512]{1,0:T(8,128)S(1)}, f32[20,64,256]{2,1,0:T(8,128)S(1)}, f32[...) custom-call(bf16[256,640]{1,0:T(8,128)(2,1)S(1)} %copy-done.4, ...), custom_call_target="tpu_custom_call" | custom-call | flops 10000000000 | bytes 40000000 | tf_op jit(solution)/shard_map/attention_first/pallas_call | solution.py:291
  24.5 0.0 collective-permute-done.refs_8_
  24.6 0.0 copy-start
  24.6 0.0 copy-start.1
  24.6 0.0 copy-start.5
  24.6 2.0 %collective-permute-start.1 = (bf16[640,512]{1,0:T(8,128)(2,1)S(1)}, bf16[640,512]{1,0:T(8,128)(2,1)S(1)}, u32[]{:S(2)}, u32[]{:S(2)}) collective-permute-start(bf16[640,512]{1,0:T(8,128)(2,1)S(1)} %collective-permute-done.refs_8_), channel_id=1, source_target_pairs={{0,4},{4,0},{1,5},{5,1},{2,6},{6,2},{3,7},{7,3}} | collective-permute-start | bytes 1966088 | tf_op jit(solution)/shard_map/ppermute | solution.py:402
  26.6 15.4 %attention_second.1 = (f32[256,640]{1,0:T(8,128)S(1)}, bf16[256,640]{1,0:T(8,128)(2,1)S(1)}) custom-call(s32[8,512]{1,0:T(8,128)S(1)} %get-tuple-element.34.table.tab_in, bf16[256,640]{1,0:T(8,128)(2,1)S(1)} %copy-done.4, f32[20,64,256]{2,1,0:T(8,128)S(1)} %get-tuple-element.35.q_in, f32[288,256]{1,0:T(8,128)S(1)} %get-tuple-element.36.ks_in, ...), custom_call_target="tpu_custom_call" | custom-call | flops 10000000000 | bytes 40000000 | tf_op jit(solution)/shard_map/attention_second/pallas_call | solution.py:320
  42.1 0.0 collective-permute-done.2.refs_10_
  42.1 0.0 collective-permute-start.6
  42.1 0.0 collective-permute-done.1.refs_9_
  42.1 0.5 %collective-permute-start.7 = (bf16[640,512]{1,0:T(8,128)(2,1)S(1)}, bf16[640,512]{1,0:T(8,128)(2,1)S(1)}, u32[]{:S(2)}, u32[]{:S(2)}) collective-permute-start(bf16[640,512]{1,0:T(8,128)(2,1)S(1)} %collective-permute-done.1.refs_9_), channel_id=1, source_target_pairs={{0,1},{1,0},{2,3},{3,2},{4,5},{5,4},{6,7},{7,6}} | collective-permute-start | bytes 1966088 | tf_op jit(solution)/shard_map/ppermute | solution.py:406
  42.6 0.0 collective-permute-done.3.refs_5_
  42.6 0.0 collective-permute-start.8
  42.7 0.0 collective-permute-done.4.refs_6_
  42.7 0.0 collective-permute-done.5.refs_7_
  42.7 2.1 %mlp.2.refs_0_ = f32[256,640]{1,0:T(8,128)S(1)} custom-call(f32[256,640]{1,0:T(8,128)S(1)} %get-tuple-element.43.refs_0_, bf16[256,640]{1,0:T(8,128)(2,1)S(1)} %get-tuple-element.44.refs_1_, bf16[640,512]{1,0:T(8,128)(2,1)S(1)} %copy-done, bf16[640,512]{1,0:T(8,128)(2,1)S(1)} %copy-done.1, bf16[512,640]{1,0:T(8,128)(2,1)S(1)} %copy-done.5, ...), custom_call_target="tpu_custom_call" | custom-call | flops 1509949440 | bytes 5898240 | tf_op jit(solution)/shard_map/mlp/pallas_call | solution.py:372
  44.8 0.0 collective-permute-done.6.refs_2_
  44.8 0.3 collective-permute-done.7.refs_3_
  45.1 0.9 %collective-permute-done.8.refs_4_ = bf16[512,640]{1,0:T(8,128)(2,1)S(1)} collective-permute-done((bf16[512,640]{1,0:T(8,128)(2,1)S(1)}, bf16[512,640]{1,0:T(8,128)(2,1)S(1)}, u32[]{:S(2)}, u32[]{:S(2)}) %collective-permute-start.8) | collective-permute-done | bytes 655392 | tf_op jit(solution)/shard_map/ppermute | solution.py:407
  46.1 1.6 %mlp.3 = bf16[256,640]{1,0:T(8,128)(2,1)} custom-call(f32[256,640]{1,0:T(8,128)S(1)} %mlp.2.refs_0_, bf16[256,640]{1,0:T(8,128)(2,1)S(1)} %get-tuple-element.44.refs_1_, bf16[640,512]{1,0:T(8,128)(2,1)S(1)} %collective-permute-done.6.refs_2_, bf16[640,512]{1,0:T(8,128)(2,1)S(1)} %collective-permute-done.7.refs_3_, ...), custom_call_target="tpu_custom_call" | custom-call | flops 503316480 | bytes 1966080 | tf_op jit(solution)/shard_map/mlp/pallas_call | solution.py:372
  (15 shorter events, 0.0 us)
Async XLA Ops:
  0.6 5.2 %copy-start.9 = (bf16[640]{0:T(1024)(128)(2,1)S(1)}, bf16[640]{0:T(1024)(128)(2,1)}, u32[]{:S(2)}) copy-start(bf16[640]{0:T(1024)(128)(2,1)} %param.17) | copy-start | bytes 3844
  0.6 5.2 %copy-start.8 = (s32[256]{0:T(256)S(1)}, s32[256]{0:T(256)}, u32[]{:S(2)}) copy-start(s32[256]{0:T(256)} %param.16) | copy-start | bytes 3076
  0.7 5.2 %copy-start.4 = (bf16[256,640]{1,0:T(8,128)(2,1)S(1)}, bf16[256,640]{1,0:T(8,128)(2,1)}, u32[]{:S(2)}) copy-start(bf16[256,640]{1,0:T(8,128)(2,1)} %x_in.3) | copy-start | bytes 983044
  0.7 5.2 %copy-start.2 = (bf16[640,1024]{1,0:T(8,128)(2,1)S(1)}, bf16[640,1024]{1,0:T(8,128)(2,1)}, u32[]{:S(2)}) copy-start(bf16[640,1024]{1,0:T(8,128)(2,1)} %wq.1) | copy-start | bytes 3932164
  0.7 5.2 %copy-start.6 = (bf16[640,256]{1,0:T(8,128)(2,1)S(1)}, bf16[640,256]{1,0:T(8,128)(2,1)}, u32[]{:S(2)}) copy-start(bf16[640,256]{1,0:T(8,128)(2,1)} %wk.1) | copy-start | bytes 983044
  0.7 42.0 %collective-permute-start.3 = (bf16[640,512]{1,0:T(8,128)(2,1)}, bf16[640,512]{1,0:T(8,128)(2,1)S(1)}, u32[]{:S(2)}, u32[]{:S(2)}) collective-permute-start(bf16[640,512]{1,0:T(8,128)(2,1)} %refs_2_.1), channel_id=1, source_target_pairs={{0,1},{1,0},{2,3},{3,2},{4,5},{5,4},{6,7},{7,6}} | collective-permute-start | bytes 1966088 | tf_op jit(solution)/shard_map/ppermute | solution.py:399
  1.6 41.1 %collective-permute-start.4 = (bf16[640,512]{1,0:T(8,128)(2,1)}, bf16[640,512]{1,0:T(8,128)(2,1)S(1)}, u32[]{:S(2)}, u32[]{:S(2)}) collective-permute-start(bf16[640,512]{1,0:T(8,128)(2,1)} %refs_3_.1), channel_id=1, source_target_pairs={{0,1},{1,0},{2,3},{3,2},{4,5},{5,4},{6,7},{7,6}} | collective-permute-start | bytes 1966088 | tf_op jit(solution)/shard_map/ppermute | solution.py:399
  2.8 21.8 %collective-permute-start = (bf16[640,512]{1,0:T(8,128)(2,1)S(1)}, bf16[640,512]{1,0:T(8,128)(2,1)S(1)}, u32[]{:S(2)}, u32[]{:S(2)}) collective-permute-start(bf16[640,512]{1,0:T(8,128)(2,1)S(1)} %broadcast_select_fusion), channel_id=1, source_target_pairs={{0,2},{1,3},{2,0},{3,1},{4,6},{5,7},{6,4},{7,5}} | collective-permute-start | bytes 1966088 | tf_op jit(solution)/shard_map/ppermute | solution.py:396
  5.8 36.9 %collective-permute-start.5 = (bf16[512,640]{1,0:T(8,128)(2,1)}, bf16[512,640]{1,0:T(8,128)(2,1)S(1)}, u32[]{:S(2)}, u32[]{:S(2)}) collective-permute-start(bf16[512,640]{1,0:T(8,128)(2,1)} %refs_4_.1), channel_id=1, source_target_pairs={{0,1},{1,0},{2,3},{3,2},{4,5},{5,4},{6,7},{7,6}} | collective-permute-start | bytes 1966088 | tf_op jit(solution)/shard_map/ppermute | solution.py:399
  5.8 36.3 %collective-permute-start.2 = (bf16[512,640]{1,0:T(8,128)(2,1)}, bf16[512,640]{1,0:T(8,128)(2,1)S(1)}, u32[]{:S(2)}, u32[]{:S(2)}) collective-permute-start(bf16[512,640]{1,0:T(8,128)(2,1)} %refs_4_.1), channel_id=1, source_target_pairs={{0,2},{1,3},{2,0},{3,1},{4,6},{5,7},{6,4},{7,5}} | collective-permute-start | bytes 1966088 | tf_op jit(solution)/shard_map/ppermute | solution.py:398
  5.9 1.0 %copy-start.7 = (bf16[640,256]{1,0:T(8,128)(2,1)S(1)}, bf16[640,256]{1,0:T(8,128)(2,1)}, u32[]{:S(2)}) copy-start(bf16[640,256]{1,0:T(8,128)(2,1)} %wv.1) | copy-start | bytes 983044
  6.9 17.7 %copy-start.10 = (bf16[640]{0:T(1024)(128)(2,1)S(1)}, bf16[640]{0:T(1024)(128)(2,1)}, u32[]{:S(2)}) copy-start(bf16[640]{0:T(1024)(128)(2,1)} %param.18) | copy-start | bytes 3844
  6.9 19.8 %copy-start.3 = (bf16[1024,640]{1,0:T(8,128)(2,1)S(1)}, bf16[1024,640]{1,0:T(8,128)(2,1)}, u32[]{:S(2)}) copy-start(bf16[1024,640]{1,0:T(8,128)(2,1)} %wo.1) | copy-start | bytes 3932164
  24.6 18.1 %copy-start = (bf16[640,512]{1,0:T(8,128)(2,1)S(1)}, bf16[640,512]{1,0:T(8,128)(2,1)}, u32[]{:S(2)}) copy-start(bf16[640,512]{1,0:T(8,128)(2,1)} %refs_2_.1) | copy-start | bytes 1966084
  24.6 18.1 %copy-start.1 = (bf16[640,512]{1,0:T(8,128)(2,1)S(1)}, bf16[640,512]{1,0:T(8,128)(2,1)}, u32[]{:S(2)}) copy-start(bf16[640,512]{1,0:T(8,128)(2,1)} %refs_3_.1) | copy-start | bytes 1966084
  24.6 18.1 %copy-start.5 = (bf16[512,640]{1,0:T(8,128)(2,1)S(1)}, bf16[512,640]{1,0:T(8,128)(2,1)}, u32[]{:S(2)}) copy-start(bf16[512,640]{1,0:T(8,128)(2,1)} %refs_4_.1) | copy-start | bytes 1966084
  24.6 17.5 %collective-permute-start.1 = (bf16[640,512]{1,0:T(8,128)(2,1)S(1)}, bf16[640,512]{1,0:T(8,128)(2,1)S(1)}, u32[]{:S(2)}, u32[]{:S(2)}) collective-permute-start(bf16[640,512]{1,0:T(8,128)(2,1)S(1)} %collective-permute-done.refs_8_), channel_id=1, source_target_pairs={{0,4},{4,0},{1,5},{5,1},{2,6},{6,2},{3,7},{7,3}} | collective-permute-start | bytes 1966088 | tf_op jit(solution)/shard_map/ppermute | solution.py:402
  42.1 2.7 %collective-permute-start.6 = (bf16[640,512]{1,0:T(8,128)(2,1)S(1)}, bf16[640,512]{1,0:T(8,128)(2,1)S(1)}, u32[]{:S(2)}, u32[]{:S(2)}) collective-permute-start(bf16[640,512]{1,0:T(8,128)(2,1)S(1)} %collective-permute-done.refs_8_), channel_id=1, source_target_pairs={{0,1},{1,0},{2,3},{3,2},{4,5},{5,4},{6,7},{7,6}} | collective-permute-start | bytes 1966088 | tf_op jit(solution)/shard_map/ppermute | solution.py:403
  42.1 3.0 %collective-permute-start.7 = (bf16[640,512]{1,0:T(8,128)(2,1)S(1)}, bf16[640,512]{1,0:T(8,128)(2,1)S(1)}, u32[]{:S(2)}, u32[]{:S(2)}) collective-permute-start(bf16[640,512]{1,0:T(8,128)(2,1)S(1)} %collective-permute-done.1.refs_9_), channel_id=1, source_target_pairs={{0,1},{1,0},{2,3},{3,2},{4,5},{5,4},{6,7},{7,6}} | collective-permute-start | bytes 1966088 | tf_op jit(solution)/shard_map/ppermute | solution.py:406
  42.6 3.5 %collective-permute-start.8 = (bf16[512,640]{1,0:T(8,128)(2,1)S(1)}, bf16[512,640]{1,0:T(8,128)(2,1)S(1)}, u32[]{:S(2)}, u32[]{:S(2)}) collective-permute-start(bf16[512,640]{1,0:T(8,128)(2,1)S(1)} %collective-permute-done.2.refs_10_), channel_id=1, source_target_pairs={{0,1},{1,0},{2,3},{3,2},{4,5},{5,4},{6,7},{7,6}} | collective-permute-start | bytes 1966088 | tf_op jit(solution)/shard_map/ppermute | solution.py:407
